TPU v7x, 32 devices: a 4x4x1 block of a 4x4x8 slice. The times are simulated.
32 devices in a mesh: data: 1 (over z), img: 4 (over y), seq: 8 (over x, core).
Axes of the slice: x: 4, y: 4, z: 1, core: 2. Of those that a mesh axis runs over, the one named last changes fastest.
The devices are a block of a 4x4x8 slice.
Arguments:
- x_in: bfloat16 [4, 32768, 384], P(('data', 'img'), 'seq')
- grad_y: bfloat16 [4, 32768, 384], P(('data', 'img'), 'seq')
- ln_gamma: float32 [384], replicated
- ln_beta: float32 [384], replicated
- w_qkv: bfloat16 [384, 1152], replicated
- w_out: bfloat16 [384, 384], replicated
- head_temp: float32 [8], replicated
Outputs:
- output 1: bfloat16 [4, 32768, 384], P(('data', 'img'), 'seq')
- output 2: bfloat16 [4, 32768, 384], P(('data', 'img'), 'seq')
- output 3: float32 [384, 1152], P(('data', 'seq'))
- output 4: float32 [384, 384], P(('data', 'seq'))
- output 5: float32 [384], P('data')
- output 6: float32 [384], P('data')
- output 7: float32 [8], P('data')
All inputs are finite; a program needn't handle non-finite values.
Results may differ from a plain program's by a relative error of at most 0.00309468.
Values are sent between devices in bfloat16 or wider.
A program may use at most 768 MiB of HBM per device.

v0:
```python
import jax
import jax.numpy as jnp
from jax import lax
from jax.sharding import PartitionSpec as P

LN_EPS = 1e-6


def layer_norm(x_f32, ln_gamma, ln_beta):
    row_mean = jnp.mean(x_f32, axis=-1, keepdims=True)
    centered = x_f32 - row_mean
    row_var = jnp.mean(centered * centered, axis=-1, keepdims=True)
    return centered * lax.rsqrt(row_var + LN_EPS) * ln_gamma + ln_beta


def attn_probs(gram_mat, sum_qq, sum_kk, head_temp):
    scale_mat = head_temp[..., :, None, None] * lax.rsqrt(sum_qq)[..., :, None] * lax.rsqrt(sum_kk)[..., None, :]
    return jax.nn.softmax(gram_mat * scale_mat, axis=-1)


def solution(mesh):
    act_spec = P(('data', 'img'), 'seq', None)
    row_spec = P(('data', 'seq'), None)
    in_specs = (act_spec, act_spec, P(), P(), P(), P(), P())
    out_specs = (act_spec, act_spec, row_spec, row_spec, P('data'), P('data'), P('data'))

    def local_block(x_in, grad_y, ln_gamma, ln_beta, w_qkv, w_out, head_temp):
        x_loc = x_in[0]
        gy_loc = grad_y[0]
        n_tok, model_dim = x_loc.shape
        n_heads = head_temp.shape[0]
        head_dim = model_dim // n_heads
        w_qkv4 = w_qkv.reshape(model_dim, 3, n_heads, head_dim)
        x_f32 = x_loc.astype(jnp.float32)
        u_f32, ln_pull = jax.vjp(layer_norm, x_f32, ln_gamma, ln_beta)
        u_act = u_f32.astype(jnp.bfloat16)
        qkv_all = jnp.einsum('nd,dchi->cnhi', u_act, w_qkv4, preferred_element_type=jnp.float32).astype(jnp.bfloat16)
        q_act = qkv_all[0]
        k_act = qkv_all[1]
        v_act = qkv_all[2]
        gram_part = jnp.einsum('nhi,nhj->hij', q_act, k_act, preferred_element_type=jnp.float32)
        sqq_part = jnp.sum(jnp.square(q_act.astype(jnp.float32)), axis=0)
        skk_part = jnp.sum(jnp.square(k_act.astype(jnp.float32)), axis=0)
        gram_mat, sum_qq, sum_kk = lax.psum((gram_part, sqq_part, skk_part), 'seq')
        attn_p, attn_pull = jax.vjp(attn_probs, gram_mat, sum_qq, sum_kk, head_temp)
        attn_pb = attn_p.astype(jnp.bfloat16)
        head_out = jnp.einsum('nhj,hij->nhi', v_act, attn_pb, preferred_element_type=jnp.float32).astype(jnp.bfloat16).reshape(n_tok, model_dim)
        proj_out = jnp.dot(head_out, w_out, preferred_element_type=jnp.float32)
        y_loc = (x_f32 + proj_out).astype(jnp.bfloat16)
        grad_o = jnp.einsum('ne,de->nd', gy_loc, w_out, preferred_element_type=jnp.float32).astype(jnp.bfloat16).reshape(n_tok, n_heads, head_dim)
        attn_part = jnp.einsum('nhi,nhj->hij', grad_o, v_act, preferred_element_type=jnp.float32)
        grad_attn = lax.psum(attn_part, 'seq')
        grad_v = jnp.einsum('nhi,hij->nhj', grad_o, attn_pb, preferred_element_type=jnp.float32)
        grad_gram, grad_sqq, grad_skk, grad_temp_img = attn_pull(grad_attn)
        gram_gb = grad_gram.astype(jnp.bfloat16)
        grad_q = jnp.einsum('nhj,hij->nhi', k_act, gram_gb, preferred_element_type=jnp.float32) + 2.0 * grad_sqq * q_act
        grad_k = jnp.einsum('nhi,hij->nhj', q_act, gram_gb, preferred_element_type=jnp.float32) + 2.0 * grad_skk * k_act
        grad_qkv = jnp.stack([grad_q, grad_k, grad_v]).astype(jnp.bfloat16)
        grad_u = jnp.einsum('cnhi,dchi->nd', grad_qkv, w_qkv4, preferred_element_type=jnp.float32).astype(jnp.bfloat16)
        grad_xln, gam_loc, bet_loc = ln_pull(grad_u.astype(jnp.float32))
        grad_x = (gy_loc.astype(jnp.float32) + grad_xln).astype(jnp.bfloat16)
        wqkv_loc = jnp.einsum('nd,cnhi->dchi', u_act, grad_qkv, preferred_element_type=jnp.float32).reshape(model_dim, 3 * model_dim)
        wout_loc = jnp.einsum('nd,ne->de', head_out, gy_loc, preferred_element_type=jnp.float32)
        grad_wqkv = lax.psum(lax.psum_scatter(wqkv_loc, 'seq', scatter_dimension=0, tiled=True), 'img')
        grad_wout = lax.psum(lax.psum_scatter(wout_loc, 'seq', scatter_dimension=0, tiled=True), 'img')
        grad_gamma, grad_beta = lax.psum((gam_loc, bet_loc), ('img', 'seq'))
        grad_temp = lax.psum(grad_temp_img, 'img')
        return y_loc[None], grad_x[None], grad_wqkv, grad_wout, grad_gamma, grad_beta, grad_temp

    return jax.shard_map(local_block, mesh=mesh, in_specs=in_specs, out_specs=out_specs, check_vma=False)
```

profile of v0, /device:TPU:97, one launch (start us, length us, event | category | flops | bytes accessed | tf_op | source)
XLA Modules:
  0.0 258.7 jit_solution(706781904833580465)
XLA Ops:
  7.3 2.7 %convert_reduce_fusion.1 = f32[4096]{0:T(1024)S(1)} fusion(bf16[1,4096,384]{2,1,0:T(8,128)(2,1)} %param.7), kind=kLoop, calls=%fused_computation.6 | loop fusion | flops 3141632 | bytes 3162112 | tf_op jit(solution)/shard_map/jvp()/reduce_sum | solution.py:10
  10.0 3.0 %fusion.14 = f32[4096]{0:T(1024)S(1)} fusion(bf16[1,4096,384]{2,1,0:T(8,128)(2,1)} %param.7, f32[4096]{0:T(1024)S(1)} %broadcast_multiply_fusion), kind=kLoop, calls=%fused_computation.27 | loop fusion | flops 6287360 | bytes 3178496 | tf_op jit(solution)/shard_map/jvp()/reduce_sum | solution.py:12
  13.1 5.4 %fusion.49 = f32[4096,1152]{0,1:S(1)} fusion(bf16[384,1152]{1,0:T(8,128)(2,1)S(1)} %copy-done.7, bf16[1,4096,384]{2,1,0:T(8,128)(2,1)S(1)} %copy-done.2, f32[384]{0:T(512)S(1)} %copy-done.10, f32[384]{0:T(512)S(1)} %copy-done.8, f32[4096]{0:T(1024)S(1)} %fusion.42, f32[4096]{0:T(1024)S(1)} %broadcast_multiply_fusion), kind=kOutput, calls=%fused_computation.83 | convolution fusion | flops 3633315840 | bytes 22940672
  18.4 1.4 convert_bitcast_fusion.1
  19.8 1.6 fusion.33
  21.5 2.6 copy-done.3
  24.1 1.8 convolution_convert_fusion.2
  25.9 1.6 copy-done.5
  27.6 2.0 fusion.32
  29.7 3.5 %fusion.8 = (f32[8,48]{1,0:T(8,128)S(1)}, f32[8,48]{1,0:T(8,128)S(1)}) fusion(bf16[3,4096,8,48]{1,3,2,0:T(8,128)(2,1)} %copy-done.1), kind=kLoop, calls=%fused_computation.21 | loop fusion | flops 9436416 | bytes 6294528 | tf_op jit(solution)/shard_map/reduce_sum | solution.py:42
  33.2 14.2 %all-reduce.1 = (f32[8,48]{1,0:T(8,128)S(1)}, f32[8,48]{1,0:T(8,128)S(1)}) all-reduce(f32[8,48]{1,0:T(8,128)S(1)} %get-tuple-element.8, f32[8,48]{1,0:T(8,128)S(1)} %get-tuple-element.7), channel_id=1, replica_groups=mesh['data'=1,'img'=4,'seq'=8] {'seq'}, use_global_device_ids=true, to_apply=%region_6.0 | all-reduce | flops 768 | bytes 6144 | tf_op jit(solution)/shard_map/psum | solution.py:44
  47.5 2.2 copy.18
  49.7 37.4 %all-reduce.7.cloned.1.call-done = (f32[8,48,48]{2,1,0:T(8,128)}, f32[8,48,48]{2,1,0:T(8,128)}) async-done(((f32[8,48,48]{2,1,0:T(8,128)}, f32[8,48,48]{2,1,0:T(8,128)}), (f32[8,48,48]{2,1,0:T(8,128)}, f32[8,48,48]{2,1,0:T(8,128)})) %all-reduce.7.cloned.1.call-update) | async-done | bytes 147472 | tf_op jit(solution)/shard_map/psum | solution.py:44
  87.2 2.0 fusion.51
  89.2 5.3 %convolution_convert_fusion.1 = bf16[8,48,4096]{2,1,0:T(8,128)(2,1)} fusion(bf16[3,4096,8,48]{1,3,2,0:T(8,128)(2,1)} %copy-done.1, f32[8,48]{1,0:T(8,128)S(1)} %get-tuple-element.26, f32[8,48,48]{2,1,0:T(8,128)} %get-tuple-element.19, f32[8,48]{1,0:T(8,128)S(1)} %rsqrt.18, f32[8,48]{1,0:T(8,128)S(1)} %rsqrt_multiply_fusion.1), kind=kOutput, calls=%fused_computation.38 | convolution fusion | flops 152660400 | bytes 6492672 | tf_op jit(solution)/shard_map/nhj,hij->nhi/dot_general | solution.py:47
  94.5 5.2 %fusion.22 = bf16[1,4096,8,48]{1,3,2,0:T(8,128)(2,1)} fusion(bf16[4096,8,48]{0,2,1:T(8,128)(2,1)} %bitcast.112, f32[8,48]{1,0:T(8,128)S(1)} %get-tuple-element.26, f32[8,48,48]{2,1,0:T(8,128)} %get-tuple-element.19, f32[8,48]{1,0:T(8,128)S(1)} %rsqrt.18, f32[8,48]{1,0:T(8,128)S(1)} %rsqrt_multiply_fusion.1), kind=kOutput, calls=%fused_computation.40 | convolution fusion | flops 152660400 | bytes 6369792 | tf_op jit(solution)/shard_map/nhi,hij->nhj/dot_general | solution.py:53
  99.7 1.3 multiply_reduce_fusion.2
  101.0 1.4 multiply_reduce_fusion.1
  102.6 6.0 %fusion.24 = bf16[1,4096,8,48]{1,3,2,0:T(8,128)(2,1)} fusion(f32[8,48]{1,0:T(8,128)S(1)} %multiply_multiply_fusion.4, bf16[3,4096,8,48]{1,3,2,0:T(8,128)(2,1)} %copy-done.1, f32[8,48,48]{2,1,0:T(8,128)S(1)} %get-tuple-element.23, f32[8,48]{1,0:T(8,128)S(1)} %rsqrt.18, f32[8,48]{1,0:T(8,128)S(1)} %rsqrt_multiply_fusion.1), kind=kOutput, calls=%fused_computation.42 | convolution fusion | flops 157341696 | bytes 9515520 | tf_op jit(solution)/shard_map/nhi,hij->nhj/dot_general | solution.py:57
  108.6 5.8 %fusion.25 = bf16[1,4096,8,48]{1,3,2,0:T(8,128)(2,1)} fusion(f32[8,48]{1,0:T(8,128)S(1)} %get-tuple-element.25, bf16[3,4096,8,48]{1,3,2,0:T(8,128)(2,1)} %copy-done.1, f32[8,48,48]{2,1,0:T(8,128)S(1)} %get-tuple-element.23, f32[8,48]{1,0:T(8,128)S(1)} %rsqrt.18, f32[8,48]{1,0:T(8,128)S(1)} %rsqrt_multiply_fusion.1), kind=kOutput, calls=%fused_computation.43 | convolution fusion | flops 157341696 | bytes 9515520 | tf_op jit(solution)/shard_map/nhj,hij->nhi/dot_general | solution.py:56
  114.4 2.6 %fusion.29 = f32[384,384]{1,0:T(8,128)} fusion(bf16[4096,384]{0,1:T(8,128)(2,1)S(1)} %bitcast.115, bf16[1,4096,384]{2,1,0:T(8,128)(2,1)S(1)} %copy-done.4), kind=kOutput, calls=%fused_computation.50 | convolution fusion | flops 1207959552 | bytes 6881280 | tf_op jit(solution)/shard_map/nd,ne->de/dot_general | solution.py:63
  117.4 8.4 %pad_maximum_fusion = bf16[3,4096,8,48]{1,3,2,0:T(8,128)(2,1)} fusion(bf16[1,4096,8,48]{1,3,2,0:T(8,128)(2,1)} %fusion.22, bf16[1,4096,8,48]{1,3,2,0:T(8,128)(2,1)} %fusion.24, bf16[1,4096,8,48]{1,3,2,0:T(8,128)(2,1)} %fusion.25), kind=kLoop, calls=%fused_computation.8 | loop fusion | flops 9437184 | bytes 18874368 | tf_op jit(solution)/shard_map/stack | solution.py:58
  125.8 10.3 %fusion.47 = f32[384,1152]{1,0:T(8,128)} fusion(bf16[1152,4096]{1,0:T(8,128)(2,1)} %bitcast.113, bf16[1,4096,384]{2,1,0:T(8,128)(2,1)S(1)} %copy-done.2, f32[384]{0:T(512)S(1)} %copy-done.10, f32[384]{0:T(512)S(1)} %copy-done.8, f32[4096]{0:T(1024)S(1)} %fusion.42, f32[4096]{0:T(1024)S(1)} %broadcast_multiply_fusion), kind=kOutput, calls=%fused_computation.82 | convolution fusion | flops 3633315840 | bytes 14388224 | tf_op jit(solution)/shard_map/nd,cnhi->dchi/dot_general | solution.py:62
  136.2 10.8 %convert_reduce_fusion = (f32[384]{0:T(512)S(1)}, f32[4096]{0:T(1024)S(1)}, bf16[4096,384]{1,0:T(8,128)(2,1)}) fusion(f32[384]{0:T(512)S(1)} %copy-done.8, f32[4096]{0:T(1024)S(1)} %broadcast_multiply_fusion, bf16[1,4096,384]{2,1,0:T(8,128)(2,1)S(1)} %copy-done.2, bf16[384,3,8,48]{0,3,2,1:T(8,128)(2,1)} %bitcast.116, bf16[1,4096,8,48]{1,3,2,0:T(8,128)(2,1)} %fusion.22, ...), kind=kOutput, calls=%fused_computation.2 | convolution fusion | flops 3645894144 | bytes 16649216 | tf_op jit(solution)/shard_map/cnhi,dchi->nd/dot_general | solution.py:59
  147.0 9.0 %psum.71 = f32[8]{0:T(128)} all-reduce(f32[8]{0:T(128)S(1)} %get-tuple-element.24), channel_id=1, replica_groups=mesh['data'=1,'img'=4,'seq'=8] {'img'}, use_global_device_ids=true, to_apply=%region_24.0 | all-reduce | flops 8 | bytes 64 | tf_op jit(solution)/shard_map/psum | solution.py:67
  156.0 4.9 %fusion.21 = (f32[384]{0:T(512)S(1)}, f32[4096]{0:T(1024)S(1)}) fusion(bf16[4096,384]{1,0:T(8,128)(2,1)} %get-tuple-element.28, bf16[1,4096,384]{2,1,0:T(8,128)(2,1)S(1)} %copy-done.2, f32[4096]{0:T(1024)S(1)} %fusion.42, f32[4096]{0:T(1024)S(1)} %broadcast_multiply_fusion, f32[4096]{0:T(1024)S(1)} %multiply_multiply_fusion.3, f32[384]{0:T(512)S(1)} %copy-done.8), kind=kLoop, calls=%fused_computation.34 | loop fusion | flops 18869888 | bytes 6360064 | tf_op jit(solution)/shard_map/transpose(jvp())/reduce_sum | solution.py:13
  160.9 46.9 %all-reduce = (f32[384]{0:T(512)}, f32[384]{0:T(512)}) all-reduce(f32[384]{0:T(512)S(1)} %get-tuple-element.9, f32[384]{0:T(512)S(1)} %get-tuple-element.11), channel_id=1, replica_groups=mesh['data'=1,'img'=4,'seq'=8] {'img','seq'}, use_global_device_ids=true, to_apply=%region_20.0 | all-reduce | flops 768 | bytes 6144 | tf_op jit(solution)/shard_map/psum | solution.py:66
  207.8 7.3 %fusion.27 = bf16[1,4096,384]{2,1,0:T(8,128)(2,1)} fusion(bf16[1,4096,384]{2,1,0:T(8,128)(2,1)S(1)} %copy-done.2, bf16[4096,384]{1,0:T(8,128)(2,1)} %get-tuple-element.28, bf16[1,4096,384]{2,1,0:T(8,128)(2,1)} %param.8, f32[4096]{0:T(1024)S(1)} %negate_multiply_fusion, f32[4096]{0:T(1024)S(1)} %multiply_multiply_fusion.3, f32[4096]{0:T(1024)S(1)} %fusion.42, ...), kind=kLoop, calls=%fused_computation.45 | loop fusion | flops 18874368 | bytes 12649984 | tf_op jit(solution)/shard_map/broadcast_in_dim | solution.py:68
  215.2 5.7 %fusion.23 = bf16[1,4096,384]{2,1,0:T(8,128)(2,1)} fusion(bf16[4096,384]{0,1:T(8,128)(2,1)} %bitcast.114, bf16[384,384]{1,0:T(8,128)(2,1)S(1)} %copy-done, bf16[1,4096,384]{2,1,0:T(8,128)(2,1)S(1)} %copy-done.2), kind=kOutput, calls=%fused_computation.41 | convolution fusion | flops 1212678144 | bytes 9732096 | tf_op jit(solution)/shard_map/dot_general | solution.py:48
  220.9 28.1 %all-reduce.9.cloned.1.call-done = (f32[48,1152]{1,0:T(8,128)}, f32[48,384]{1,0:T(8,128)}) async-done(((f32[48,1152]{1,0:T(8,128)}, f32[48,384]{1,0:T(8,128)}), (f32[48,1152]{1,0:T(8,128)}, f32[48,384]{1,0:T(8,128)})) %all-reduce.9.cloned.1.call-update) | async-done | bytes 294928 | tf_op jit(solution)/shard_map/psum | solution.py:64
  249.0 1.6 copy.28
  250.6 1.5 copy.29
  (40 shorter events, 1.0 us)
Async XLA Ops:
  7.2 14.3 %copy-start = (bf16[384,384]{1,0:T(8,128)(2,1)S(1)}, bf16[384,384]{1,0:T(8,128)(2,1)}, u32[]{:S(2)}) copy-start(bf16[384,384]{1,0:T(8,128)(2,1)} %param.12) | copy-start | bytes 884740
  7.2 5.8 %copy-start.2 = (bf16[1,4096,384]{2,1,0:T(8,128)(2,1)S(1)}, bf16[1,4096,384]{2,1,0:T(8,128)(2,1)}, u32[]{:S(2)}) copy-start(bf16[1,4096,384]{2,1,0:T(8,128)(2,1)} %param.7) | copy-start | bytes 9437188
  7.2 5.8 %copy-start.10 = (f32[384]{0:T(512)S(1)}, f32[384]{0:T(512)}, u32[]{:S(2)}) copy-start(f32[384]{0:T(512)} %param.10) | copy-start | bytes 4612
  7.2 5.8 %copy-start.8 = (f32[384]{0:T(512)S(1)}, f32[384]{0:T(512)}, u32[]{:S(2)}) copy-start(f32[384]{0:T(512)} %param.9) | copy-start | bytes 4612
  7.2 79.9 %all-reduce.7.cloned.1.call-start = ((), (), s32[]{:S(2)}) async-start(), calls=%async_computation.4 | async-start | bytes 786432 | tf_op jit(solution)/shard_map/psum | solution.py:44
  7.3 5.8 %copy-start.7 = (bf16[384,1152]{1,0:T(8,128)(2,1)S(1)}, bf16[384,1152]{1,0:T(8,128)(2,1)}, u32[]{:S(2)}) copy-start(bf16[384,1152]{1,0:T(8,128)(2,1)} %param.11) | copy-start | bytes 2654212
  19.8 6.1 %copy-start.1 = (bf16[3,4096,8,48]{1,3,2,0:T(8,128)(2,1)}, bf16[3,4096,8,48]{1,3,2,0:T(8,128)(2,1)S(1)}, u32[]{:S(2)}) copy-start(bf16[3,4096,8,48]{1,3,2,0:T(8,128)(2,1)S(1)} %convert_bitcast_fusion.1) | copy-start | bytes 28311556
  19.8 4.2 %copy-start.3 = (bf16[1,4096,384]{2,1,0:T(8,128)(2,1)S(1)}, bf16[1,4096,384]{2,1,0:T(8,128)(2,1)}, u32[]{:S(2)}) copy-start(bf16[1,4096,384]{2,1,0:T(8,128)(2,1)} %param.8) | copy-start | bytes 9437188
  25.9 1.7 copy-start.5
  27.6 19.9 %copy-start.9 = (f32[8]{0:T(128)S(1)}, f32[8]{0:T(128)}, u32[]{:S(2)}) copy-start(f32[8]{0:T(128)} %param.13) | copy-start | bytes 100
  29.6 185.5 %reduce-scatter.5.cloned.1.call-start = ((), (), s32[]{:S(2)}) async-start(), calls=%async_computation.3 | async-start | bytes 663552 | tf_op jit(solution)/shard_map/reduce_scatter | solution.py:65
  102.6 11.8 %copy-start.4 = (bf16[1,4096,384]{2,1,0:T(8,128)(2,1)S(1)}, bf16[1,4096,384]{2,1,0:T(8,128)(2,1)}, u32[]{:S(2)}) copy-start(bf16[1,4096,384]{2,1,0:T(8,128)(2,1)} %param.8) | copy-start | bytes 9437188
  102.6 11.8 %copy-start.6 = (bf16[8,48,4096]{2,1,0:T(8,128)(2,1)S(1)}, bf16[8,48,4096]{2,1,0:T(8,128)(2,1)}, u32[]{:S(2)}) copy-start(bf16[8,48,4096]{2,1,0:T(8,128)(2,1)} %convolution_convert_fusion.1) | copy-start | bytes 9437188
  117.1 98.1 %reduce-scatter.3.cloned.1.call-start = ((), (), s32[]{:S(2)}) async-start(), calls=%async_computation.2 | async-start | bytes 1990656 | tf_op jit(solution)/shard_map/reduce_scatter | solution.py:64
  136.2 112.8 %all-reduce.9.cloned.1.call-start = ((), (), s32[]{:S(2)}) async-start(), calls=%async_computation.5 | async-start | bytes 589824 | tf_op jit(solution)/shard_map/psum | solution.py:64
Sparse Core Ops, SparseCore 0:
  29.7 57.3 all-reduce.6
  117.2 27.3 reduce-scatter.4
  146.9 29.5 reduce-scatter.2
  215.3 33.6 all-reduce.8
where the time goes:
time: 261 us; the launch traced here: 259 us
  blocking collectives  70.1 us (27%)
  waiting for transfers between devices  65.7 us (25%)
  matrix products  62.6 us (24%)
  other arithmetic  36.1 us (14%)
  between operations  14 us (5%)
  local copies, waits for them, and re-layouts  9.66 us (4%)
    psum x1, blocking collectives, local_block(): grad_gamma, grad_beta = lax.psum((gam_loc, bet_loc), ('img', 'seq'))  46.9 us
    psum x1, waiting for transfers between devices, local_block(): gram_mat, sum_qq, sum_kk = lax.psum((gram_part, sqq_part, skk_part), 'seq')  37.4 us
    psum x1, waiting for transfers between devices, local_block(): lax.psum(lax.psum_scatter(wqkv_loc, 'seq', scatter_dimension=0, tiled=Tru...  28.1 us
    psum x1, blocking collectives, local_block(): gram_mat, sum_qq, sum_kk = lax.psum((gram_part, sqq_part, skk_part), 'seq')  14.2 us
    dot_general x1, matrix products, local_block(): jnp.einsum('cnhi,dchi->nd', grad_qkv, w_qkv4, preferred_element_type=jnp....  10.8 us
    dot_general x1, matrix products, local_block(): jnp.einsum('nd,cnhi->dchi', u_act, grad_qkv, preferred_element_type=jnp.f...  10.3 us
    unnamed x25, local copies, waits for them, and re-layouts  9.66 us
    psum x1, blocking collectives, local_block(): grad_temp = lax.psum(grad_temp_img, 'img')  9.01 us
  transfers between devices with their start and end apart: 4, of which 2 were waited for; matrix products, arithmetic and copies ran while one was open for 21% of the time, Pallas kernels for 0%

commit v1 on v0

v1 whole, which is shorter than its diff:
```python
import functools

import jax
import jax.numpy as jnp
from jax import lax
from jax.experimental import pallas as pl
from jax.experimental.pallas import tpu as pltpu
from jax.sharding import PartitionSpec as P

LN_EPS = 1e-6
BF = jnp.bfloat16
F32 = jnp.float32
MESH = pl.DeviceIdType.MESH
WIN = 256
LANES = 128
SUB = 256


def _dot(a, b):
    return lax.dot_general(a, b, (((1,), (0,)), ((), ())), preferred_element_type=F32)


def _dot_nt(a, b):
    return lax.dot_general(a, b, (((1,), (1,)), ((), ())), preferred_element_type=F32)


def _column(row):
    return jnp.transpose(jnp.broadcast_to(row, (LANES, row.shape[1])))


def _twice(x):
    return jnp.concatenate([x, x], axis=1)


def _kernel(cfg, x_hbm, gy_hbm, gam_hbm, bet_hbm, wqkv_hbm, wout_hbm, tau_ref,
            y_hbm, gx_hbm, dwqkv_ref, dwout_ref, dgam_ref, dbet_ref, dtau_ref,
            x_v, gy_v, x_t, gy_t, u_t, q_t, k_t, v_t, do_t, o_t, dqkv_t,
            mean_v, rstd_v, w_v, w_t, wo_v, wo_t, gam_v, bet_v, gam_c, bet_c,
            g_lo, g_hi, da_lo, da_hi, sq_acc, sk_acc, dgam_acc, dbet_acc,
            a_f32, scale_f32, g_f32, a_lo, a_hi, at_lo, at_hi, dg_lo, dg_hi, dgt_lo, dgt_hi,
            cq_c, ck_c, srow, rqcol,
            ex1_src, ex1_rc, ex1_x, ex1_fin, ex2_src, ex2_rc, ex2_x, ex2_fin,
            acc_e, acc_l, d2d_e, d2d_l, rs_e, rs_l, ag_e, ag_l,
            gb_src, gb_rc, gb_all,
            x_sem, gy_sem, y_sem, gx_sem, w_sem,
            ex1_ss, ex1_rs, ex2_ss, ex2_rs,
            d2d_ss, d2d_rs, rs_ss, rs_rs, ag_ss, ag_rs, gb_ss, gb_rs):
    n_chip, n_img, n_blk, blk, dim, n_head = cfg
    hd = dim // n_head
    n_lo = WIN // hd
    r_lo = n_lo * hd
    hi0 = dim - WIN
    off_hi = r_lo - hi0
    r_hi = dim - r_lo
    n_sub = blk // SUB
    inv_d = 1.0 / dim
    data_i = lax.axis_index('data')
    img_i = lax.axis_index('img')
    seq_i = lax.axis_index('seq')
    core = lax.rem(seq_i, 2)
    chip = seq_i // 2

    def dev(chip_to, core_to, img_to):
        return (data_i, img_to, chip_to * 2 + core_to)

    partner = dev(chip, 1 - core, img_i)

    def rcopy(src, dst, ssem, rsem, to):
        return pltpu.make_async_remote_copy(src_ref=src, dst_ref=dst, send_sem=ssem, recv_sem=rsem,
                                            device_id=to, device_id_type=MESH)

    offsets = [(dc, di) for dc in range(n_chip) for di in range(n_img) if (dc, di) != (0, 0)]

    def peer(dc, di):
        return lax.rem(chip + dc, n_chip), lax.rem(img_i + di, n_img)

    def x_copy(i):
        return pltpu.make_async_copy(x_hbm.at[0, pl.ds(i * blk, blk), :], x_v.at[i], x_sem.at[i])

    def gy_copy(i):
        return pltpu.make_async_copy(gy_hbm.at[0, pl.ds(i * blk, blk), :], gy_v.at[i], gy_sem.at[i])

    def y_copy(i):
        return pltpu.make_async_copy(x_v.at[i], y_hbm.at[0, pl.ds(i * blk, blk), :], y_sem.at[i])

    def gx_copy(i):
        return pltpu.make_async_copy(gy_v.at[i], gx_hbm.at[0, pl.ds(i * blk, blk), :], gx_sem.at[i])

    small = [(gam_hbm, gam_v), (bet_hbm, bet_v), (wqkv_hbm, w_v), (wout_hbm, wo_v)]
    loads = [pltpu.make_async_copy(s, d, w_sem.at[n]) for n, (s, d) in enumerate(small)]
    loads[0].start()
    loads[1].start()
    x_copy(0).start()
    loads[2].start()
    for i in range(1, n_blk):
        x_copy(i).start()
    loads[3].start()
    for i in range(n_blk):
        gy_copy(i).start()

    barrier = pltpu.get_barrier_semaphore()
    pl.semaphore_signal(barrier, inc=1, device_id=partner, device_id_type=MESH)
    for dc, di in offsets:
        pc, pi = peer(dc, di)
        pl.semaphore_signal(barrier, inc=1, device_id=dev(pc, core, pi), device_id_type=MESH)

    for ref in (g_lo, g_hi, da_lo, da_hi, sq_acc, sk_acc, dgam_acc, dbet_acc, acc_e, acc_l):
        ref[...] = jnp.zeros_like(ref)

    loads[0].wait()
    loads[1].wait()
    gam_c[...] = _column(gam_v[...])
    bet_c[...] = _column(bet_v[...])
    loads[2].wait()
    for c in range(3):
        w_t[c * dim:(c + 1) * dim, :] = jnp.transpose(w_v[:, c * dim:(c + 1) * dim])
    loads[3].wait()
    wo_t[...] = jnp.transpose(wo_v[...])

    def sub(n):
        return slice(n * SUB, (n + 1) * SUB)

    def body_qk(i, _):
        x_copy(i).wait()
        for n in range(n_sub):
            x_t[i, :, sub(n)] = jnp.transpose(x_v[i, sub(n), :])
        for c in range(blk // LANES):
            cols = slice(c * LANES, (c + 1) * LANES)
            xs = x_t[i, :, cols].astype(F32)
            mean = jnp.sum(xs, axis=0, keepdims=True) * inv_d
            cen = xs - mean
            var = jnp.sum(cen * cen, axis=0, keepdims=True) * inv_d
            rstd = lax.rsqrt(var + LN_EPS)
            mean_v[i, :, cols] = mean
            rstd_v[i, :, cols] = rstd
            u_t[i, :, cols] = (cen * rstd * gam_c[...] + bet_c[...]).astype(BF)
        for n in range(n_sub):
            u_n = u_t[i, :, sub(n)]
            for part, ref, acc in ((0, q_t, sq_acc), (1, k_t, sk_acc)):
                r = _dot(w_t[part * dim:(part + 1) * dim, :], u_n).astype(BF)
                ref[i, :, sub(n)] = r
                rf = r.astype(F32)
                rf = rf * rf
                acc[...] += rf[:, :LANES] + rf[:, LANES:]
        g_lo[...] += _dot_nt(q_t[i, :r_lo, :], k_t[i, :WIN, :])
        g_hi[...] += _dot_nt(q_t[i, r_lo:, :], k_t[i, hi0:, :])
        return 0

    lax.fori_loop(0, n_blk, body_qk, 0)

    def pack(lo, hi, put):
        col = lax.broadcasted_iota(jnp.int32, (hd, WIN), 1)
        t_lo = jnp.zeros((hd, WIN), F32)
        for h in range(n_lo):
            t_lo += jnp.where((col >= h * hd) & (col < (h + 1) * hd), lo[h * hd:(h + 1) * hd, :], 0.0)
        t_hi = jnp.zeros((hd, WIN), F32)
        for h in range(n_lo, n_head):
            b = h * hd - hi0
            r = h * hd - r_lo
            t_hi += jnp.where((col >= b) & (col < b + hd), hi[r:r + hd, :], 0.0)
        put(jnp.concatenate([t_lo[:, :hi0], t_lo[:, hi0:] + t_hi[:, :WIN - hi0], t_hi[:, WIN - hi0:]], axis=1))

    def ex_pair(src, rc, ss, rs):
        return rcopy(src.at[1 - core], rc, ss.at[0], rs.at[0], partner)

    def ex_chip(buf, ss, rs, dc):
        return rcopy(buf.at[chip], buf.at[chip], ss.at[dc], rs.at[dc], dev(lax.rem(chip + dc, n_chip), core, img_i))

    def ex_swap(fin, ss, rs):
        return rcopy(fin.at[core], fin.at[core], ss.at[n_chip], rs.at[n_chip], partner)

    def ex_step2(src, rc, buf, ss, rs):
        ex_pair(src, rc, ss, rs).wait()
        buf[chip] = src[core] + rc[...]
        for dc in range(1, n_chip):
            ex_chip(buf, ss, rs, dc).start()

    def ex_step3(buf, fin, ss, rs):
        for dc in range(1, n_chip):
            ex_chip(buf, ss, rs, dc).wait()
        tot = buf[0]
        for j in range(1, n_chip):
            tot += buf[j]
        fin[core] = tot
        ex_swap(fin, ss, rs).start()

    def put_g(t):
        h1 = ex1_src.shape[1]
        sq = jnp.sum(jnp.transpose(sq_acc[...]), axis=0, keepdims=True)
        sk = jnp.sum(jnp.transpose(sk_acc[...]), axis=0, keepdims=True)
        ex1_src[0] = t[:h1]
        ex1_src[1, :hd - h1] = t[h1:]
        ex1_src[1, hd - h1:hd - h1 + 8] = jnp.broadcast_to(sq, (8, dim))
        ex1_src[1, hd - h1 + 8:] = jnp.broadcast_to(sk, (8, dim))

    def put_da(t):
        ex2_src[0] = t[:hd // 2]
        ex2_src[1] = t[hd // 2:]

    pack(g_lo, g_hi, put_g)
    pl.semaphore_wait(barrier, 1 + len(offsets))
    ex_pair(ex1_src, ex1_rc, ex1_ss, ex1_rs).start()

    def body_v(i, _):
        gy_copy(i).wait()
        for n in range(n_sub):
            gy_t[i, :, sub(n)] = jnp.transpose(gy_v[i, sub(n), :])
        for n in range(n_sub):
            v_t[i, :, sub(n)] = _dot(w_t[2 * dim:, :], u_t[i, :, sub(n)]).astype(BF)
            do_t[i, :, sub(n)] = _dot(wo_v[...], gy_t[i, :, sub(n)]).astype(BF)
        da_lo[...] += _dot_nt(do_t[i, :r_lo, :], v_t[i, :WIN, :])
        da_hi[...] += _dot_nt(do_t[i, r_lo:, :], v_t[i, hi0:, :])

        @pl.when(i == 0)
        def _():
            ex_step2(ex1_src, ex1_rc, ex1_x, ex1_ss, ex1_rs)
        return 0

    lax.fori_loop(0, n_blk, body_v, 0)

    pack(da_lo, da_hi, put_da)
    ex_pair(ex2_src, ex2_rc, ex2_ss, ex2_rs).start()
    ex_step3(ex1_x, ex1_fin, ex1_ss, ex1_rs)
    ex_swap(ex1_fin, ex1_ss, ex1_rs).wait()

    def head_mask(rows, row0, col0):
        r = lax.broadcasted_iota(jnp.int32, (rows, WIN), 0) + row0
        c = lax.broadcasted_iota(jnp.int32, (rows, WIN), 1) + col0
        out = (r < 0)
        for h in range(n_head):
            out |= (r >= h * hd) & (r < (h + 1) * hd) & (c >= h * hd) & (c < (h + 1) * hd)
        return out

    windows = ((0, r_lo, 0, n_lo), (r_lo, r_hi, hi0, n_head - n_lo))
    h1 = ex1_fin.shape[1]
    gcat = jnp.concatenate([ex1_fin[0], ex1_fin[1, :hd - h1]], axis=0)
    sq = ex1_fin[1, hd - h1:hd - h1 + 1]
    sk = ex1_fin[1, hd - h1 + 8:hd - h1 + 9]
    rk = lax.rsqrt(sk)
    srow[0:1] = sk
    srow[1:2] = rk
    sq_c = _column(sq)
    rq_c = lax.rsqrt(sq_c)
    rqcol[0] = sq_c
    rqcol[1] = rq_c
    tau_c = jnp.concatenate([jnp.full((hd, LANES), tau_ref[h], F32) for h in range(n_head)], axis=0)
    rqcol[2] = tau_c
    for w, (row0, rows, col0, heads) in enumerate(windows):
        g = jnp.concatenate([gcat[:, col0:col0 + WIN]] * heads, axis=0)
        mask = head_mask(rows, row0, col0)
        scale = _twice((tau_c * rq_c)[row0:row0 + rows]) * rk[:, col0:col0 + WIN]
        s = g * scale
        top = jnp.max(jnp.where(mask, s, -jnp.inf), axis=1, keepdims=True)
        e = jnp.where(mask, jnp.exp(jnp.where(mask, s - top, 0.0)), 0.0)
        a = e / jnp.sum(e, axis=1, keepdims=True)
        a_f32[row0:row0 + rows] = a
        scale_f32[row0:row0 + rows] = scale
        g_f32[row0:row0 + rows] = g
        if w == 0:
            full = jnp.concatenate([a, jnp.zeros((WIN - rows, WIN), F32)], axis=0)
            a_lo[...] = full.astype(BF)
            at_lo[...] = jnp.transpose(full).astype(BF)
        else:
            full = jnp.concatenate([jnp.zeros((WIN - rows, WIN), F32), a], axis=0)
            a_hi[...] = full.astype(BF)
            at_hi[...] = jnp.transpose(full).astype(BF)

    ex_step2(ex2_src, ex2_rc, ex2_x, ex2_ss, ex2_rs)

    def add_rows(acc, g, val):
        rb = dim // (2 * n_chip)
        n_a = n_img // 2
        rc = rb // n_a
        for s in range(2 * n_chip):
            for a in range(n_a):
                acc[s % 2, s // 2, 2 * a + g] += val[s * rb + a * rc:s * rb + (a + 1) * rc]

    def body_ov(i, _):
        for n in range(n_sub):
            o_t[i, :r_lo, sub(n)] = _dot(a_lo[:r_lo], v_t[i, :WIN, sub(n)]).astype(BF)
            o_t[i, r_lo:, sub(n)] = _dot(a_hi[off_hi:], v_t[i, hi0:, sub(n)]).astype(BF)
            dqkv_t[i, 2 * dim:2 * dim + r_lo, sub(n)] = _dot(at_lo[:r_lo], do_t[i, :WIN, sub(n)]).astype(BF)
            dqkv_t[i, 2 * dim + r_lo:, sub(n)] = _dot(at_hi[off_hi:], do_t[i, hi0:, sub(n)]).astype(BF)
        add_rows(acc_e, 0, _dot(o_t[i], gy_v[i]))
        add_rows(acc_e, 1, _dot_nt(u_t[i], dqkv_t[i, 2 * dim:, :]))
        return 0

    lax.fori_loop(0, n_blk, body_ov, 0)

    def pair_copy(r, acc, buf):
        return rcopy(acc.at[1 - core], buf, d2d_ss.at[r], d2d_rs.at[r], partner)

    def rs_copy(r, acc, buf, n):
        pc, pi = peer(*offsets[n])
        return rcopy(acc.at[core, pc, pi], buf.at[n], rs_ss.at[r, n], rs_rs.at[r, n], dev(pc, core, pi))

    def ag_copy(r, buf, di):
        return rcopy(buf.at[img_i], buf.at[img_i], ag_ss.at[r, di], ag_rs.at[r, di],
                     dev(chip, core, lax.rem(img_i + di, n_img)))

    def rs_start(r, acc, buf, rbuf):
        pair_copy(r, acc, buf).wait()
        for j in range(n_chip):
            acc[core, j] += buf[j]
        for n in range(len(offsets)):
            rs_copy(r, acc, rbuf, n).start()

    def rs_finish(r, acc, rbuf, gbuf):
        tot = acc[core, chip, img_i]
        for n in range(len(offsets)):
            rs_copy(r, acc, rbuf, n).wait()
            tot += rbuf[n]
        gbuf[img_i] = tot
        for di in range(1, n_img):
            ag_copy(r, gbuf, di).start()

    pair_copy(0, acc_e, d2d_e).start()
    ex_step3(ex2_x, ex2_fin, ex2_ss, ex2_rs)
    ex_swap(ex2_fin, ex2_ss, ex2_rs).wait()

    dacat = jnp.concatenate([ex2_fin[0], ex2_fin[1]], axis=0)
    sq_c = rqcol[0]
    rq_c = rqcol[1]
    tau_c = rqcol[2]
    sk = srow[0:1]
    rk = srow[1:2]
    row_sums = []
    col_sums = []
    for w, (row0, rows, col0, heads) in enumerate(windows):
        da = jnp.concatenate([dacat[:, col0:col0 + WIN]] * heads, axis=0)
        a = a_f32[row0:row0 + rows]
        ds = a * (da - jnp.sum(a * da, axis=1, keepdims=True))
        dg = ds * scale_f32[row0:row0 + rows]
        dscale = ds * g_f32[row0:row0 + rows]
        row_sums.append(jnp.broadcast_to(jnp.sum(dscale * rk[:, col0:col0 + WIN], axis=1, keepdims=True),
                                         (rows, LANES)))
        col_sums.append(jnp.sum(dscale * _twice((tau_c * rq_c)[row0:row0 + rows]), axis=0, keepdims=True))
        if w == 0:
            full = jnp.concatenate([dg, jnp.zeros((WIN - rows, WIN), F32)], axis=0)
            dg_lo[...] = full.astype(BF)
            dgt_lo[...] = jnp.transpose(full).astype(BF)
        else:
            full = jnp.concatenate([jnp.zeros((WIN - rows, WIN), F32), dg], axis=0)
            dg_hi[...] = full.astype(BF)
            dgt_hi[...] = jnp.transpose(full).astype(BF)
    t_row = jnp.concatenate(row_sums, axis=0)
    cl, ch = col_sums
    w_col = jnp.concatenate([cl[:, :hi0], cl[:, hi0:] + ch[:, :WIN - hi0], ch[:, WIN - hi0:]], axis=1)
    cq_c[...] = 2.0 * (-0.5 * rq_c / sq_c * (tau_c * t_row))
    ck_c[...] = _column(2.0 * (-0.5 * rk / sk * w_col))
    lane = lax.broadcasted_iota(jnp.int32, (1, LANES), 1)
    dtau_row = jnp.zeros((1, LANES), F32)
    for h in range(n_head):
        part = jnp.sum((rq_c * t_row)[h * hd:(h + 1) * hd], axis=0, keepdims=True)
        dtau_row += jnp.where(lane == h, part, 0.0)
    gb_src[6:7] = jnp.where(seq_i == 0, dtau_row, 0.0)
    gb_src[7:8] = jnp.zeros((1, LANES), F32)

    rs_start(0, acc_e, d2d_e, rs_e)

    def body_qk_back(i, _):
        for n in range(n_sub):
            k_n = k_t[i, :, sub(n)]
            q_n = q_t[i, :, sub(n)]
            dq = jnp.concatenate([_dot(dg_lo[:r_lo], k_n[:WIN]), _dot(dg_hi[off_hi:], k_n[hi0:])], axis=0)
            dqkv_t[i, :dim, sub(n)] = (dq + _twice(cq_c[...]) * q_n.astype(F32)).astype(BF)
            dk = jnp.concatenate([_dot(dgt_lo[:r_lo], q_n[:WIN]), _dot(dgt_hi[off_hi:], q_n[hi0:])], axis=0)
            dqkv_t[i, dim:2 * dim, sub(n)] = (dk + _twice(ck_c[...]) * k_n.astype(F32)).astype(BF)
        dw = _dot_nt(u_t[i], dqkv_t[i, :2 * dim, :])
        add_rows(acc_l, 0, dw[:, :dim])
        add_rows(acc_l, 1, dw[:, dim:])
        return 0

    lax.fori_loop(0, n_blk, body_qk_back, 0)
    pair_copy(1, acc_l, d2d_l).start()

    def body_y(i, _):
        for n in range(n_sub):
            proj = _dot(wo_t[...], o_t[i, :, sub(n)])
            x_v[i, sub(n), :] = jnp.transpose((x_t[i, :, sub(n)].astype(F32) + proj).astype(BF))
        y_copy(i).start()
        return 0

    lax.fori_loop(0, n_blk, body_y, 0)
    rs_start(1, acc_l, d2d_l, rs_l)
    rs_finish(0, acc_e, rs_e, ag_e)

    def body_x(i, _):
        for n in range(n_sub):
            du = _dot(w_v[...], dqkv_t[i, :, sub(n)]).astype(BF)
            for c in range(SUB // LANES):
                cols = slice(n * SUB + c * LANES, n * SUB + (c + 1) * LANES)
                du_c = du[:, c * LANES:(c + 1) * LANES].astype(F32)
                rstd = rstd_v[i, :, cols]
                xh = (x_t[i, :, cols].astype(F32) - mean_v[i, :, cols]) * rstd
                dgam_acc[...] += du_c * xh
                dbet_acc[...] += du_c
                g = du_c * gam_c[...]
                c1 = jnp.sum(g, axis=0, keepdims=True) * inv_d
                c2 = jnp.sum(g * xh, axis=0, keepdims=True) * inv_d
                gx = gy_t[i, :, cols].astype(F32) + rstd * (g - c1 - xh * c2)
                gy_v[i, cols, :] = jnp.transpose(gx.astype(BF))
        gx_copy(i).start()
        return 0

    lax.fori_loop(0, n_blk, body_x, 0)

    for b, acc in ((0, dgam_acc), (3, dbet_acc)):
        row = jnp.sum(jnp.transpose(acc[...]), axis=0, keepdims=True)
        for c in range(dim // LANES):
            gb_src[b + c:b + c + 1] = row[:, c * LANES:(c + 1) * LANES]
    gb_pair = rcopy(gb_src, gb_rc, gb_ss.at[0], gb_rs.at[0], partner)
    gb_pair.start()

    rs_finish(1, acc_l, rs_l, ag_l)

    gb_pair.wait()
    gb_all[chip, img_i] = gb_src[...] + gb_rc[...]

    def gb_copy(n):
        pc, pi = peer(*offsets[n])
        return rcopy(gb_all.at[chip, img_i], gb_all.at[chip, img_i], gb_ss.at[1 + n], gb_rs.at[1 + n],
                     dev(pc, core, pi))

    for n in range(len(offsets)):
        gb_copy(n).start()

    def emit(r, gbuf, outs):
        for di in range(1, n_img):
            ag_copy(r, gbuf, di).wait()
        rc = gbuf.shape[1]
        for a in range(n_img // 2):
            for g, (ref, col) in enumerate(outs):
                ref[a * rc:(a + 1) * rc, col:col + dim] = gbuf[2 * a + g]

    emit(0, ag_e, ((dwout_ref, 0), (dwqkv_ref, 2 * dim)))
    for n in range(len(offsets)):
        gb_copy(n).wait()
    tot = jnp.zeros(gb_src.shape, F32)
    for j in range(n_chip):
        for m in range(n_img):
            tot += gb_all[j, m]
    for c in range(dim // LANES):
        dgam_ref[:, c * LANES:(c + 1) * LANES] = tot[c:c + 1]
        dbet_ref[:, c * LANES:(c + 1) * LANES] = tot[3 + c:4 + c]
    dtau_ref[...] = tot[6:7]
    emit(1, ag_l, ((dwqkv_ref, 0), (dwqkv_ref, dim)))
    for i in range(n_blk):
        y_copy(i).wait()
        gx_copy(i).wait()


def solution(mesh):
    act_spec = P(('data', 'img'), 'seq', None)
    row_spec = P(('data', 'seq'), None)
    in_specs = (act_spec, act_spec, P(), P(), P(), P(), P())
    out_specs = (act_spec, act_spec, row_spec, row_spec, P('data'), P('data'), P('data'))
    n_img = mesh.shape['img']
    n_seq = mesh.shape['seq']
    n_chip = n_seq // 2

    def local_block(x_in, grad_y, ln_gamma, ln_beta, w_qkv, w_out, head_temp):
        _, n_tok, dim = x_in.shape
        n_head = head_temp.shape[0]
        hd = dim // n_head
        blk = min(1024, n_tok)
        n_blk = n_tok // blk
        rb = dim // n_seq
        rc = rb // (n_img // 2)
        h1 = (hd + 16) // 2
        hbm = pl.BlockSpec(memory_space=pl.ANY)
        vmem = pl.BlockSpec(memory_space=pltpu.VMEM)
        smem = pl.BlockSpec(memory_space=pltpu.SMEM)
        V = pltpu.VMEM
        n_off = n_chip * n_img - 1
        n_hi = n_head - WIN // hd
        r_hi = n_hi * hd
        r_lo = dim - r_hi
        feat = V((n_blk, dim, blk), BF)
        tok = V((n_blk, blk, dim), BF)
        stat = V((n_blk, 1, blk), F32)
        col = V((dim, LANES), F32)
        sqr = V((WIN, WIN), BF)
        acc = V((2, n_chip, n_img, rc, dim), F32)
        dma = pltpu.SemaphoreType.DMA
        scratch = [
            tok, tok, feat, feat, feat, feat, feat, feat, feat, feat, V((n_blk, 3 * dim, blk), BF),
            stat, stat, V((dim, 3 * dim), BF), V((3 * dim, dim), BF), V((dim, dim), BF), V((dim, dim), BF),
            V((1, dim), F32), V((1, dim), F32), col, col,
            V((r_lo, WIN), F32), V((r_hi, WIN), F32), V((r_lo, WIN), F32), V((r_hi, WIN), F32),
            col, col, col, col,
            V((dim, WIN), F32), V((dim, WIN), F32), V((dim, WIN), F32),
            sqr, sqr, sqr, sqr, sqr, sqr, sqr, sqr,
            col, col, V((8, dim), F32), V((3, dim, LANES), F32),
            V((2, h1, dim), F32), V((h1, dim), F32), V((n_chip, h1, dim), F32), V((2, h1, dim), F32),
            V((2, hd // 2, dim), F32), V((hd // 2, dim), F32), V((n_chip, hd // 2, dim), F32),
            V((2, hd // 2, dim), F32),
            acc, acc, V((n_chip, n_img, rc, dim), F32), V((n_chip, n_img, rc, dim), F32),
            V((n_off, rc, dim), F32), V((n_off, rc, dim), F32), V((n_img, rc, dim), F32), V((n_img, rc, dim), F32),
            V((8, LANES), F32), V((8, LANES), F32), V((n_chip, n_img, 8, LANES), F32),
            dma((n_blk,)), dma((n_blk,)), dma((n_blk,)), dma((n_blk,)), dma((4,)),
            dma((n_chip + 1,)), dma((n_chip + 1,)), dma((n_chip + 1,)), dma((n_chip + 1,)),
            dma((2,)), dma((2,)), dma((2, n_off)), dma((2, n_off)), dma((2, n_img)), dma((2, n_img)),
            dma((1 + n_off,)), dma((1 + n_off,)),
        ]
        out_shape = (
            jax.ShapeDtypeStruct(x_in.shape, BF), jax.ShapeDtypeStruct(x_in.shape, BF),
            jax.ShapeDtypeStruct((rb, 3 * dim), F32), jax.ShapeDtypeStruct((rb, dim), F32),
            jax.ShapeDtypeStruct((1, dim), F32), jax.ShapeDtypeStruct((1, dim), F32),
            jax.ShapeDtypeStruct((1, LANES), F32),
        )
        cfg = (n_chip, n_img, n_blk, blk, dim, n_head)
        y, gx, dwqkv, dwout, dgam, dbet, dtau = pl.pallas_call(
            functools.partial(_kernel, cfg),
            out_shape=out_shape,
            in_specs=[hbm, hbm, hbm, hbm, hbm, hbm, smem],
            out_specs=(hbm, hbm, vmem, vmem, vmem, vmem, vmem),
            scratch_shapes=scratch,
            compiler_params=pltpu.CompilerParams(collective_id=0, has_side_effects=True,
                                                 vmem_limit_bytes=62 * 1024 * 1024),
        )(x_in, grad_y, ln_gamma.reshape(1, dim), ln_beta.reshape(1, dim), w_qkv, w_out, head_temp)
        return (y, gx, dwqkv, dwout, dgam.reshape(dim), dbet.reshape(dim), dtau[0, :n_head])

    return jax.shard_map(local_block, mesh=mesh, in_specs=in_specs, out_specs=out_specs, check_vma=False)
```

time: 261 us -> 71.6 us (0.27)
  blocking collectives: 70.1 us -> 0 us
  waiting for transfers between devices: 65.7 us -> 0 us
  matrix products: 62.6 us -> 0 us
  Pallas kernels: 0 us -> 57.6 us
  other arithmetic: 36.1 us -> 2.47 us
  between operations: 14 us -> 0.65 us
    psum x3 -> x0, blocking collectives: 70.1 us -> none  [the longest x1 46.9 us: local_block(): grad_gamma, grad_beta = lax.psum((gam_loc, bet_loc), ('img', 'seq'))]
    psum x2 -> x0, waiting for transfers between devices: 65.5 us -> none  [the longest x1 37.4 us: local_block(): gram_mat, sum_qq, sum_kk = lax.psum((gram_part, sqq_part, skk_part), 'seq')]
    pallas_call x0 -> x1, Pallas kernels: none -> 57.6 us  [local_block(): pl.pallas_call(functools.partial(_kernel, cfg), out_shape=out_shape, in_s...]
    dot_general x11 -> x0, matrix products: 57.2 us -> none  [the longest x1 10.8 us: local_block(): jnp.einsum('cnhi,dchi->nd', grad_qkv, w_qkv4, preferred_element_type=jnp....]
    reduce_sum x7 -> x0, other arithmetic: 16.9 us -> none  [the longest x1 4.87 us: layer_norm(): return centered * lax.rsqrt(row_var + LN_EPS) * ln_gamma + ln_beta]
    another operation x1 -> x0, other arithmetic: 8.39 us -> none  [local_block(): grad_qkv = jnp.stack([grad_q, grad_k, grad_v]).astype(jnp.bfloat16)]
    broadcast_in_dim x1 -> x0, other arithmetic: 7.33 us -> none  [local_block(): grad_x[None]]
    unnamed x1 -> x0, matrix products: 5.36 us -> none
  transfers between devices with their start and end apart: 4 -> 0, of which waited for: 2 -> 0; matrix products, arithmetic and copies ran while one was open for 21% -> 0% of each run, Pallas kernels for 0% -> 0%
where the time goes in v1:
time: 71.6 us; the launch traced here: 71.4 us
  Pallas kernels  57.6 us (80%)
  local copies, waits for them, and re-layouts  10.6 us (15%)
  other arithmetic  2.47 us (3%)
    pallas_call x1, Pallas kernels, local_block(): pl.pallas_call(functools.partial(_kernel, cfg), out_shape=out_shape, in_s...  57.6 us
    unnamed x10, local copies, waits for them, and re-layouts  7.01 us
    pallas_call x2, other arithmetic, local_block(): pl.pallas_call(functools.partial(_kernel, cfg), out_shape=out_shape, in_s...  2.47 us

profile of v1, /device:TPU:97, one launch (start us, length us, event | category | flops | bytes accessed | tf_op | source)
XLA Modules:
  0.0 71.4 jit_solution(2139235254681207538)
XLA Ops:
  0.6 1.2 %reshape.26.gam_hbm = f32[1,384]{1,0:T(1,128)} reshape(f32[384]{0:T(512)} %param.9) | data formatting | bytes 3072 | tf_op jit(solution)/shard_map/reshape | solution.py:521
  1.9 1.2 %reshape.27.bet_hbm = f32[1,384]{1,0:T(1,128)} reshape(f32[384]{0:T(512)} %param.10) | data formatting | bytes 3072 | tf_op jit(solution)/shard_map/reshape | solution.py:521
  3.1 57.6 %shard_map.126 = (bf16[1,4096,384]{2,1,0:T(8,128)(2,1)}, bf16[1,4096,384]{2,1,0:T(8,128)(2,1)}, f32[48,1152]{1,0:T(8,128)}, f32[48,384]{1,0:T(8,128)}, f32[1,384...) custom-call(bf16[1,4096,384]{2,1,0:T(8,128)(2,1)} %x_hbm.1, bf16[1,4096,384]{2,1,0:T(8,128)(2,1)} %gy_hbm.1, ...), custom_call_target="tpu_custom_call" | custom-call | tf_op jit(solution)/shard_map/pallas_call | solution.py:513
  60.8 1.2 %reduce = f32[384]{0:T(512)} reduce(f32[1,384]{1,0:T(1,128)} %get-tuple-element.18, f32[]{:T(128)} %constant.2), dimensions={0}, to_apply=%get-tuple-element.18.reduce_sub_computation | reduce | bytes 3076 | tf_op jit(solution)/shard_map/pallas_call | solution.py:513
  62.0 1.2 %reduce.1 = f32[384]{0:T(512)} reduce(f32[1,384]{1,0:T(1,128)} %get-tuple-element.19, f32[]{:T(128)} %constant.2), dimensions={0}, to_apply=%get-tuple-element.19.reduce_sub_computation | reduce | bytes 3076 | tf_op jit(solution)/shard_map/pallas_call | solution.py:513
  63.2 1.1 %slice_bitcast_fusion = f32[8]{0:T(128)} fusion(f32[1,128]{1,0:T(1,128)} %get-tuple-element.20), kind=kLoop, calls=%fused_computation | loop fusion | bytes 64 | tf_op jit(solution)/shard_map/squeeze | solution.py:522
  64.4 0.0 copy-start
  64.4 4.0 %copy.18 = bf16[1,4096,384]{2,1,0:T(8,128)(2,1)} copy(bf16[1,4096,384]{2,1,0:T(8,128)(2,1)} %get-tuple-element.28) | data formatting | bytes 6291456
  68.4 0.0 copy-done
  68.4 0.0 copy-start.1
  68.4 0.0 copy-start.2
  68.4 1.7 %copy.19 = bf16[1,4096,384]{2,1,0:T(8,128)(2,1)} copy(bf16[1,4096,384]{2,1,0:T(8,128)(2,1)S(1)} %copy-done) | data formatting | bytes 6291456
  70.1 0.0 copy-done.1
  70.1 0.7 copy.20
  70.8 0.0 copy-done.2
  70.8 0.6 copy.21
Async XLA Ops:
  64.4 4.0 %copy-start = (bf16[1,4096,384]{2,1,0:T(8,128)(2,1)S(1)}, bf16[1,4096,384]{2,1,0:T(8,128)(2,1)}, u32[]{:S(2)}) copy-start(bf16[1,4096,384]{2,1,0:T(8,128)(2,1)} %get-tuple-element.29) | copy-start | bytes 9437188
  68.4 1.7 %copy-start.1 = (f32[48,1152]{1,0:T(8,128)S(1)}, f32[48,1152]{1,0:T(8,128)}, u32[]{:S(2)}) copy-start(f32[48,1152]{1,0:T(8,128)} %get-tuple-element.30) | copy-start | bytes 663556
  68.4 2.4 %copy-start.2 = (f32[48,384]{1,0:T(8,128)S(1)}, f32[48,384]{1,0:T(8,128)}, u32[]{:S(2)}) copy-start(f32[48,384]{1,0:T(8,128)} %get-tuple-element.31) | copy-start | bytes 221188

commit v2 on v1

--- a/solution.py
+++ b/solution.py
@@ -14,6 +14,7 @@
 WIN = 256
 LANES = 128
 SUB = 256
+VMEM_MAIN = 56 * 1024 * 1024
 
 
 def _dot(a, b):
@@ -33,8 +34,8 @@
 
 
 def _kernel(cfg, x_hbm, gy_hbm, gam_hbm, bet_hbm, wqkv_hbm, wout_hbm, tau_ref,
-            y_hbm, gx_hbm, dwqkv_ref, dwout_ref, dgam_ref, dbet_ref, dtau_ref,
-            x_v, gy_v, x_t, gy_t, u_t, q_t, k_t, v_t, do_t, o_t, dqkv_t,
+            x_v, gy_v, dwqkv_ref, dwout_ref, dgam_ref, dbet_ref, dtau_ref,
+            x_t, gy_t, u_t, q_t, k_t, v_t, do_t, o_t, dqkv_t,
             mean_v, rstd_v, w_v, w_t, wo_v, wo_t, gam_v, bet_v, gam_c, bet_c,
             g_lo, g_hi, da_lo, da_hi, sq_acc, sk_acc, dgam_acc, dbet_acc,
             a_f32, scale_f32, g_f32, a_lo, a_hi, at_lo, at_hi, dg_lo, dg_hi, dgt_lo, dgt_hi,
@@ -42,7 +43,7 @@
             ex1_src, ex1_rc, ex1_x, ex1_fin, ex2_src, ex2_rc, ex2_x, ex2_fin,
             acc_e, acc_l, d2d_e, d2d_l, rs_e, rs_l, ag_e, ag_l,
             gb_src, gb_rc, gb_all,
-            x_sem, gy_sem, y_sem, gx_sem, w_sem,
+            x_sem, gy_sem, w_sem,
             ex1_ss, ex1_rs, ex2_ss, ex2_rs,
             d2d_ss, d2d_rs, rs_ss, rs_rs, ag_ss, ag_rs, gb_ss, gb_rs):
     n_chip, n_img, n_blk, blk, dim, n_head = cfg
@@ -80,12 +81,6 @@
     def gy_copy(i):
         return pltpu.make_async_copy(gy_hbm.at[0, pl.ds(i * blk, blk), :], gy_v.at[i], gy_sem.at[i])
 
-    def y_copy(i):
-        return pltpu.make_async_copy(x_v.at[i], y_hbm.at[0, pl.ds(i * blk, blk), :], y_sem.at[i])
-
-    def gx_copy(i):
-        return pltpu.make_async_copy(gy_v.at[i], gx_hbm.at[0, pl.ds(i * blk, blk), :], gx_sem.at[i])
-
     small = [(gam_hbm, gam_v), (bet_hbm, bet_v), (wqkv_hbm, w_v), (wout_hbm, wo_v)]
     loads = [pltpu.make_async_copy(s, d, w_sem.at[n]) for n, (s, d) in enumerate(small)]
     loads[0].start()
@@ -109,8 +104,8 @@
 
     loads[0].wait()
     loads[1].wait()
-    gam_c[...] = _column(gam_v[...])
-    bet_c[...] = _column(bet_v[...])
+    gam_c[...] = _column(gam_v[...].reshape(1, dim))
+    bet_c[...] = _column(bet_v[...].reshape(1, dim))
     loads[2].wait()
     for c in range(3):
         w_t[c * dim:(c + 1) * dim, :] = jnp.transpose(w_v[:, c * dim:(c + 1) * dim])
@@ -378,7 +373,6 @@
         for n in range(n_sub):
             proj = _dot(wo_t[...], o_t[i, :, sub(n)])
             x_v[i, sub(n), :] = jnp.transpose((x_t[i, :, sub(n)].astype(F32) + proj).astype(BF))
-        y_copy(i).start()
         return 0
 
     lax.fori_loop(0, n_blk, body_y, 0)
@@ -400,7 +394,6 @@
                 c2 = jnp.sum(g * xh, axis=0, keepdims=True) * inv_d
                 gx = gy_t[i, :, cols].astype(F32) + rstd * (g - c1 - xh * c2)
                 gy_v[i, cols, :] = jnp.transpose(gx.astype(BF))
-        gx_copy(i).start()
         return 0
 
     lax.fori_loop(0, n_blk, body_x, 0)
@@ -412,8 +405,6 @@
     gb_pair = rcopy(gb_src, gb_rc, gb_ss.at[0], gb_rs.at[0], partner)
     gb_pair.start()
 
-    rs_finish(1, acc_l, rs_l, ag_l)
-
     gb_pair.wait()
     gb_all[chip, img_i] = gb_src[...] + gb_rc[...]
 
@@ -424,6 +415,7 @@
 
     for n in range(len(offsets)):
         gb_copy(n).start()
+    rs_finish(1, acc_l, rs_l, ag_l)
 
     def emit(r, gbuf, outs):
         for di in range(1, n_img):
@@ -440,14 +432,26 @@
     for j in range(n_chip):
         for m in range(n_img):
             tot += gb_all[j, m]
-    for c in range(dim // LANES):
-        dgam_ref[:, c * LANES:(c + 1) * LANES] = tot[c:c + 1]
-        dbet_ref[:, c * LANES:(c + 1) * LANES] = tot[3 + c:4 + c]
-    dtau_ref[...] = tot[6:7]
+    n_row = dim // LANES
+    for b, ref in ((0, dgam_ref), (n_row, dbet_ref)):
+        ref[...] = jnp.concatenate([tot[b + c:b + c + 1] for c in range(n_row)], axis=1).reshape(dim)
+    dtau_ref[...] = tot[6:7, :n_head].reshape(n_head)
     emit(1, ag_l, ((dwqkv_ref, 0), (dwqkv_ref, dim)))
-    for i in range(n_blk):
-        y_copy(i).wait()
-        gx_copy(i).wait()
+
+
+def _write(n_blk, blk, *refs):
+    srcs, dsts, act_sem, sem = refs[:7], refs[7:14], refs[14], refs[15]
+    copies = []
+    for a in range(2):
+        for i in range(n_blk):
+            copies.append(pltpu.make_async_copy(srcs[a].at[i], dsts[a].at[0, pl.ds(i * blk, blk), :],
+                                                act_sem.at[a, i]))
+    for n in range(5):
+        copies.append(pltpu.make_async_copy(srcs[2 + n], dsts[2 + n], sem.at[n]))
+    for c in copies:
+        c.start()
+    for c in copies:
+        c.wait()
 
 
 def solution(mesh):
@@ -468,7 +472,7 @@
         rb = dim // n_seq
         rc = rb // (n_img // 2)
         h1 = (hd + 16) // 2
-        hbm = pl.BlockSpec(memory_space=pl.ANY)
+        hbm = pl.BlockSpec(memory_space=pltpu.HBM)
         vmem = pl.BlockSpec(memory_space=pltpu.VMEM)
         smem = pl.BlockSpec(memory_space=pltpu.SMEM)
         V = pltpu.VMEM
@@ -477,16 +481,15 @@
         r_hi = n_hi * hd
         r_lo = dim - r_hi
         feat = V((n_blk, dim, blk), BF)
-        tok = V((n_blk, blk, dim), BF)
         stat = V((n_blk, 1, blk), F32)
         col = V((dim, LANES), F32)
         sqr = V((WIN, WIN), BF)
         acc = V((2, n_chip, n_img, rc, dim), F32)
         dma = pltpu.SemaphoreType.DMA
         scratch = [
-            tok, tok, feat, feat, feat, feat, feat, feat, feat, feat, V((n_blk, 3 * dim, blk), BF),
+            feat, feat, feat, feat, feat, feat, feat, feat, V((n_blk, 3 * dim, blk), BF),
             stat, stat, V((dim, 3 * dim), BF), V((3 * dim, dim), BF), V((dim, dim), BF), V((dim, dim), BF),
-            V((1, dim), F32), V((1, dim), F32), col, col,
+            V((dim,), F32), V((dim,), F32), col, col,
             V((r_lo, WIN), F32), V((r_hi, WIN), F32), V((r_lo, WIN), F32), V((r_hi, WIN), F32),
             col, col, col, col,
             V((dim, WIN), F32), V((dim, WIN), F32), V((dim, WIN), F32),
@@ -498,27 +501,38 @@
             acc, acc, V((n_chip, n_img, rc, dim), F32), V((n_chip, n_img, rc, dim), F32),
             V((n_off, rc, dim), F32), V((n_off, rc, dim), F32), V((n_img, rc, dim), F32), V((n_img, rc, dim), F32),
             V((8, LANES), F32), V((8, LANES), F32), V((n_chip, n_img, 8, LANES), F32),
-            dma((n_blk,)), dma((n_blk,)), dma((n_blk,)), dma((n_blk,)), dma((4,)),
+            dma((n_blk,)), dma((n_blk,)), dma((4,)),
             dma((n_chip + 1,)), dma((n_chip + 1,)), dma((n_chip + 1,)), dma((n_chip + 1,)),
             dma((2,)), dma((2,)), dma((2, n_off)), dma((2, n_off)), dma((2, n_img)), dma((2, n_img)),
             dma((1 + n_off,)), dma((1 + n_off,)),
         ]
         out_shape = (
-            jax.ShapeDtypeStruct(x_in.shape, BF), jax.ShapeDtypeStruct(x_in.shape, BF),
-            jax.ShapeDtypeStruct((rb, 3 * dim), F32), jax.ShapeDtypeStruct((rb, dim), F32),
-            jax.ShapeDtypeStruct((1, dim), F32), jax.ShapeDtypeStruct((1, dim), F32),
-            jax.ShapeDtypeStruct((1, LANES), F32),
+            V((n_blk, blk, dim), BF), V((n_blk, blk, dim), BF), V((rb, 3 * dim), F32), V((rb, dim), F32),
+            V((dim,), F32), V((dim,), F32), V((n_head,), F32),
         )
         cfg = (n_chip, n_img, n_blk, blk, dim, n_head)
-        y, gx, dwqkv, dwout, dgam, dbet, dtau = pl.pallas_call(
+        outs = pl.pallas_call(
             functools.partial(_kernel, cfg),
             out_shape=out_shape,
             in_specs=[hbm, hbm, hbm, hbm, hbm, hbm, smem],
-            out_specs=(hbm, hbm, vmem, vmem, vmem, vmem, vmem),
+            out_specs=(vmem,) * 7,
             scratch_shapes=scratch,
             compiler_params=pltpu.CompilerParams(collective_id=0, has_side_effects=True,
-                                                 vmem_limit_bytes=62 * 1024 * 1024),
-        )(x_in, grad_y, ln_gamma.reshape(1, dim), ln_beta.reshape(1, dim), w_qkv, w_out, head_temp)
-        return (y, gx, dwqkv, dwout, dgam.reshape(dim), dbet.reshape(dim), dtau[0, :n_head])
+                                                 vmem_limit_bytes=VMEM_MAIN),
+        )(x_in, grad_y, ln_gamma, ln_beta, w_qkv, w_out, head_temp)
+        finals = (
+            jax.ShapeDtypeStruct(x_in.shape, BF), jax.ShapeDtypeStruct(x_in.shape, BF),
+            jax.ShapeDtypeStruct((rb, 3 * dim), F32), jax.ShapeDtypeStruct((rb, dim), F32),
+            jax.ShapeDtypeStruct((dim,), F32), jax.ShapeDtypeStruct((dim,), F32),
+            jax.ShapeDtypeStruct((n_head,), F32),
+        )
+        return pl.pallas_call(
+            functools.partial(_write, n_blk, blk),
+            out_shape=finals,
+            in_specs=[vmem] * 7,
+            out_specs=(hbm,) * 7,
+            scratch_shapes=[dma((2, n_blk)), dma((5,))],
+            compiler_params=pltpu.CompilerParams(vmem_limit_bytes=1 << 20),
+        )(*outs)
 
     return jax.shard_map(local_block, mesh=mesh, in_specs=in_specs, out_specs=out_specs, check_vma=False)

time: 71.6 us -> 60.7 us (0.85)
  local copies, waits for them, and re-layouts: 10.6 us -> 0 us
  other arithmetic: 2.47 us -> 0 us
  Pallas kernels: 57.6 us -> 60 us
    unnamed x10 -> x0, local copies, waits for them, and re-layouts: 7.01 us -> none
    pallas_call x0 -> x1, Pallas kernels: none -> 2.88 us  [local_block(): pl.pallas_call(functools.partial(_write, n_blk, blk), out_shape=finals, i...]
    reshape x2 -> x0, local copies, waits for them, and re-layouts: 2.49 us -> none  [the longest x1 1.25 us: local_block(): ln_gamma.reshape(1, dim)]
    pallas_call x2 -> x0, other arithmetic: 2.47 us -> none  [local_block(): pl.pallas_call(functools.partial(_kernel, cfg), out_shape=out_shape, in_s...]
    squeeze x1 -> x0, local copies, waits for them, and re-layouts: 1.15 us -> none  [local_block(): dtau[0, :n_head]]
where the time goes in v2:
time: 60.7 us; the launch traced here: 60.6 us
  Pallas kernels  60 us (99%)
  between operations  0.64 us (1%)
    pallas_call x1, Pallas kernels, local_block(): pl.pallas_call(functools.partial(_kernel, cfg), out_shape=out_shape, in_s...  57.1 us
    pallas_call x1, Pallas kernels, local_block(): pl.pallas_call(functools.partial(_write, n_blk, blk), out_shape=finals, i...  2.88 us

profile of v2, /device:TPU:97, one launch (start us, length us, event | category | flops | bytes accessed | tf_op | source)
XLA Modules:
  0.0 60.6 jit_solution(3943033743785932179)
XLA Ops:
  0.6 57.1 %shard_map.126 = (bf16[4,1024,384]{2,1,0:T(8,128)(2,1)S(1)}, bf16[4,1024,384]{2,1,0:T(8,128)(2,1)S(1)}, f32[48,1152]{1,0:T(8,128)S(1)}, f32[48,384]{1,0:T(8,128)...) custom-call(bf16[1,4096,384]{2,1,0:T(8,128)(2,1)} %x_hbm.1, bf16[1,4096,384]{2,1,0:T(8,128)(2,1)} %gy_hbm.1, ...), custom_call_target="tpu_custom_call" | custom-call | tf_op jit(solution)/shard_map/pallas_call | solution.py:514
  57.8 2.9 %shard_map.127 = (bf16[1,4096,384]{2,1,0:T(8,128)(2,1)}, bf16[1,4096,384]{2,1,0:T(8,128)(2,1)}, f32[48,1152]{1,0:T(8,128)}, f32[48,384]{1,0:T(8,128)}, f32[384]{0:T(512)}, /*index=5*/f32[384]{0:T(512)}, f32[8]{0:T(128)}) custom-call(bf16[4,1024,384]{2,1,0:T(8,128)(2,1)S(1)} %get-tuple-element.14.refs_0_, ...), custom_call_target="tpu_custom_call" | custom-call | tf_op jit(solution)/shard_map/pallas_call | solution.py:529

commit v3 on v2

--- a/solution.py
+++ b/solution.py
@@ -41,11 +41,12 @@
             a_f32, scale_f32, g_f32, a_lo, a_hi, at_lo, at_hi, dg_lo, dg_hi, dgt_lo, dgt_hi,
             cq_c, ck_c, srow, rqcol,
             ex1_src, ex1_rc, ex1_x, ex1_fin, ex2_src, ex2_rc, ex2_x, ex2_fin,
-            acc_e, acc_l, d2d_e, d2d_l, rs_e, rs_l, ag_e, ag_l,
+            acc_e, acc_q, acc_k, d2d_e, d2d_q, d2d_k, ring1, ring2, yrs_e, ag_e, rs_q, rs_k, ag_q, ag_k,
             gb_src, gb_rc, gb_all,
             x_sem, gy_sem, w_sem,
             ex1_ss, ex1_rs, ex2_ss, ex2_rs,
-            d2d_ss, d2d_rs, rs_ss, rs_rs, ag_ss, ag_rs, gb_ss, gb_rs):
+            d2d_ss, d2d_rs, ring_ss, ring_rs, yrs_ss, yrs_rs, age_ss, age_rs,
+            rs_ss, rs_rs, ag_ss, ag_rs, gb_ss, gb_rs):
     n_chip, n_img, n_blk, blk, dim, n_head = cfg
     hd = dim // n_head
     n_lo = WIN // hd
@@ -99,7 +100,7 @@
         pc, pi = peer(dc, di)
         pl.semaphore_signal(barrier, inc=1, device_id=dev(pc, core, pi), device_id_type=MESH)
 
-    for ref in (g_lo, g_hi, da_lo, da_hi, sq_acc, sk_acc, dgam_acc, dbet_acc, acc_e, acc_l):
+    for ref in (g_lo, g_hi, da_lo, da_hi, sq_acc, sk_acc, dgam_acc, dbet_acc, acc_e, acc_q, acc_k):
         ref[...] = jnp.zeros_like(ref)
 
     loads[0].wait()
@@ -270,6 +271,14 @@
             for a in range(n_a):
                 acc[s % 2, s // 2, 2 * a + g] += val[s * rb + a * rc:s * rb + (a + 1) * rc]
 
+    n_ct = dim // LANES
+
+    def add_cols(acc, val):
+        rb = dim // (2 * n_chip)
+        for s in range(2 * n_chip):
+            for ct in range(n_ct):
+                acc[s % 2, s // 2, ct] += val[s * rb:(s + 1) * rb, ct * LANES:(ct + 1) * LANES]
+
     def body_ov(i, _):
         for n in range(n_sub):
             o_t[i, :r_lo, sub(n)] = _dot(a_lo[:r_lo], v_t[i, :WIN, sub(n)]).astype(BF)
@@ -285,32 +294,120 @@
     def pair_copy(r, acc, buf):
         return rcopy(acc.at[1 - core], buf, d2d_ss.at[r], d2d_rs.at[r], partner)
 
-    def rs_copy(r, acc, buf, n):
-        pc, pi = peer(*offsets[n])
-        return rcopy(acc.at[core, pc, pi], buf.at[n], rs_ss.at[r, n], rs_rs.at[r, n], dev(pc, core, pi))
-
-    def ag_copy(r, buf, di):
-        return rcopy(buf.at[img_i], buf.at[img_i], ag_ss.at[r, di], ag_rs.at[r, di],
+    hn = n_img // 2
+    right = lax.rem(chip + 1, n_chip)
+    left = lax.rem(chip + n_chip - 1, n_chip)
+    opp = lax.rem(chip + 2, n_chip)
+
+    def ring_copy(n):
+        to = dev((right, left)[n % 2], core, img_i)
+        if n == 0:
+            src, dst = acc_e.at[core, opp, pl.ds(0, hn)], ring1.at[0]
+        elif n == 1:
+            src, dst = acc_e.at[core, opp, pl.ds(hn, hn)], ring1.at[1]
+        else:
+            src, dst = acc_e.at[core, (right, left)[n % 2]], ring2.at[n % 2]
+        return rcopy(src, dst, ring_ss.at[n], ring_rs.at[n], to)
+
+    def yrs_copy(di):
+        pi = lax.rem(img_i + di, n_img)
+        return rcopy(acc_e.at[core, chip, pi], yrs_e.at[di - 1], yrs_ss.at[di - 1], yrs_rs.at[di - 1],
+                     dev(chip, core, pi))
+
+    def age_copy(di):
+        return rcopy(ag_e.at[img_i], ag_e.at[img_i], age_ss.at[di - 1], age_rs.at[di - 1],
                      dev(chip, core, lax.rem(img_i + di, n_img)))
 
-    def rs_start(r, acc, buf, rbuf):
-        pair_copy(r, acc, buf).wait()
+    def e_step1():
+        pair_copy(0, acc_e, d2d_e).wait()
         for j in range(n_chip):
-            acc[core, j] += buf[j]
-        for n in range(len(offsets)):
-            rs_copy(r, acc, rbuf, n).start()
-
-    def rs_finish(r, acc, rbuf, gbuf):
-        tot = acc[core, chip, img_i]
-        for n in range(len(offsets)):
-            rs_copy(r, acc, rbuf, n).wait()
-            tot += rbuf[n]
-        gbuf[img_i] = tot
+            acc_e[core, j] += d2d_e[j]
+        ring_copy(0).start()
+        ring_copy(1).start()
+
+    def e_step2():
+        ring_copy(0).wait()
+        ring_copy(1).wait()
+        acc_e[core, right, :hn] += ring1[0]
+        acc_e[core, left, hn:] += ring1[1]
+        ring_copy(2).start()
+        ring_copy(3).start()
+
+    def e_step3():
+        ring_copy(2).wait()
+        ring_copy(3).wait()
+        acc_e[core, chip] += ring2[0] + ring2[1]
         for di in range(1, n_img):
-            ag_copy(r, gbuf, di).start()
-
+            yrs_copy(di).start()
+
+    def e_step4():
+        tot = acc_e[core, chip, img_i]
+        for di in range(1, n_img):
+            yrs_copy(di).wait()
+            tot += yrs_e[di - 1]
+        ag_e[img_i] = tot
+        for di in range(1, n_img):
+            age_copy(di).start()
+
+    def owner(r, ct):
+        return (2 * r + ct) % n_img
+
+    def rs_copy(r, acc, buf, ct, dc):
+        pc = lax.rem(chip + dc, n_chip)
+        sl = ct // n_img
+        return rcopy(acc.at[core, pc, ct], buf.at[sl, dc, img_i], rs_ss.at[r, ct, dc], rs_rs.at[r, sl, dc, img_i],
+                     dev(pc, core, owner(r, ct)))
+
+    def each_send(r, do):
+        for dc in range(n_chip):
+            for ct in range(n_ct):
+                if dc:
+                    do(ct, dc)
+                else:
+                    pl.when(img_i != owner(r, ct))(functools.partial(do, ct, dc))
+
+    def rs_start(r, acc, d2d, buf):
+        pair_copy(1 + r, acc, d2d).wait()
+        for j in range(n_chip):
+            acc[core, j] += d2d[j]
+        each_send(r, lambda ct, dc: rs_copy(r, acc, buf, ct, dc).start())
+
+    def ag_copy(r, gbuf, ct, di):
+        return rcopy(gbuf.at[ct], gbuf.at[ct], ag_ss.at[r, ct, di - 1], ag_rs.at[r, ct],
+                     dev(chip, core, lax.rem(img_i + di, n_img)))
+
+    def rs_finish(r, acc, buf, gbuf):
+        for ct in range(n_ct):
+            @pl.when(img_i == owner(r, ct))
+            def _(ct=ct):
+                sl = ct // n_img
+                tot = acc[core, chip, ct]
+                for dc in range(n_chip):
+                    for im in range(n_img):
+                        if dc == 0 and im == owner(r, ct):
+                            continue
+                        rcopy(buf.at[sl, dc, im], buf.at[sl, dc, im], rs_ss.at[r, ct, dc], rs_rs.at[r, sl, dc, im],
+                              partner).wait_recv()
+                        tot += buf[sl, dc, im]
+                gbuf[ct] = tot
+                for di in range(1, n_img):
+                    ag_copy(r, gbuf, ct, di).start()
+
+    def rs_end(r, acc, buf, gbuf, ref, col):
+        each_send(r, lambda ct, dc: rs_copy(r, acc, buf, ct, dc).wait_send())
+        for ct in range(n_ct):
+            @pl.when(img_i == owner(r, ct))
+            def _(ct=ct):
+                for di in range(1, n_img):
+                    ag_copy(r, gbuf, ct, di).wait_send()
+
+            @pl.when(img_i != owner(r, ct))
+            def _(ct=ct):
+                ag_copy(r, gbuf, ct, 1).wait_recv()
+            ref[:, col + ct * LANES:col + (ct + 1) * LANES] = gbuf[ct]
+
+    ex_step3(ex2_x, ex2_fin, ex2_ss, ex2_rs)
     pair_copy(0, acc_e, d2d_e).start()
-    ex_step3(ex2_x, ex2_fin, ex2_ss, ex2_rs)
     ex_swap(ex2_fin, ex2_ss, ex2_rs).wait()
 
     dacat = jnp.concatenate([ex2_fin[0], ex2_fin[1]], axis=0)
@@ -351,7 +448,7 @@
     gb_src[6:7] = jnp.where(seq_i == 0, dtau_row, 0.0)
     gb_src[7:8] = jnp.zeros((1, LANES), F32)
 
-    rs_start(0, acc_e, d2d_e, rs_e)
+    e_step1()
 
     def body_qk_back(i, _):
         for n in range(n_sub):
@@ -361,13 +458,20 @@
             dqkv_t[i, :dim, sub(n)] = (dq + _twice(cq_c[...]) * q_n.astype(F32)).astype(BF)
             dk = jnp.concatenate([_dot(dgt_lo[:r_lo], q_n[:WIN]), _dot(dgt_hi[off_hi:], q_n[hi0:])], axis=0)
             dqkv_t[i, dim:2 * dim, sub(n)] = (dk + _twice(ck_c[...]) * k_n.astype(F32)).astype(BF)
-        dw = _dot_nt(u_t[i], dqkv_t[i, :2 * dim, :])
-        add_rows(acc_l, 0, dw[:, :dim])
-        add_rows(acc_l, 1, dw[:, dim:])
+        add_cols(acc_q, _dot_nt(u_t[i], dqkv_t[i, :dim, :]))
         return 0
 
     lax.fori_loop(0, n_blk, body_qk_back, 0)
-    pair_copy(1, acc_l, d2d_l).start()
+    pair_copy(1, acc_q, d2d_q).start()
+    e_step2()
+
+    def body_wk(i, _):
+        add_cols(acc_k, _dot_nt(u_t[i], dqkv_t[i, dim:2 * dim, :]))
+        return 0
+
+    lax.fori_loop(0, n_blk, body_wk, 0)
+    pair_copy(2, acc_k, d2d_k).start()
+    rs_start(0, acc_q, d2d_q, rs_q)
 
     def body_y(i, _):
         for n in range(n_sub):
@@ -376,8 +480,7 @@
         return 0
 
     lax.fori_loop(0, n_blk, body_y, 0)
-    rs_start(1, acc_l, d2d_l, rs_l)
-    rs_finish(0, acc_e, rs_e, ag_e)
+    rs_start(1, acc_k, d2d_k, rs_k)
 
     def body_x(i, _):
         for n in range(n_sub):
@@ -394,6 +497,10 @@
                 c2 = jnp.sum(g * xh, axis=0, keepdims=True) * inv_d
                 gx = gy_t[i, :, cols].astype(F32) + rstd * (g - c1 - xh * c2)
                 gy_v[i, cols, :] = jnp.transpose(gx.astype(BF))
+
+        @pl.when(i == 0)
+        def _():
+            e_step3()
         return 0
 
     lax.fori_loop(0, n_blk, body_x, 0)
@@ -415,17 +522,10 @@
 
     for n in range(len(offsets)):
         gb_copy(n).start()
-    rs_finish(1, acc_l, rs_l, ag_l)
-
-    def emit(r, gbuf, outs):
-        for di in range(1, n_img):
-            ag_copy(r, gbuf, di).wait()
-        rc = gbuf.shape[1]
-        for a in range(n_img // 2):
-            for g, (ref, col) in enumerate(outs):
-                ref[a * rc:(a + 1) * rc, col:col + dim] = gbuf[2 * a + g]
-
-    emit(0, ag_e, ((dwout_ref, 0), (dwqkv_ref, 2 * dim)))
+    rs_finish(0, acc_q, rs_q, ag_q)
+    e_step4()
+    rs_finish(1, acc_k, rs_k, ag_k)
+
     for n in range(len(offsets)):
         gb_copy(n).wait()
     tot = jnp.zeros(gb_src.shape, F32)
@@ -436,7 +536,14 @@
     for b, ref in ((0, dgam_ref), (n_row, dbet_ref)):
         ref[...] = jnp.concatenate([tot[b + c:b + c + 1] for c in range(n_row)], axis=1).reshape(dim)
     dtau_ref[...] = tot[6:7, :n_head].reshape(n_head)
-    emit(1, ag_l, ((dwqkv_ref, 0), (dwqkv_ref, dim)))
+    rs_end(0, acc_q, rs_q, ag_q, dwqkv_ref, 0)
+    for di in range(1, n_img):
+        age_copy(di).wait()
+    rc = ag_e.shape[1]
+    for a in range(hn):
+        for g, (ref, col) in enumerate(((dwout_ref, 0), (dwqkv_ref, 2 * dim))):
+            ref[a * rc:(a + 1) * rc, col:col + dim] = ag_e[2 * a + g]
+    rs_end(1, acc_k, rs_k, ag_k, dwqkv_ref, dim)
 
 
 def _write(n_blk, blk, *refs):
@@ -485,6 +592,9 @@
         col = V((dim, LANES), F32)
         sqr = V((WIN, WIN), BF)
         acc = V((2, n_chip, n_img, rc, dim), F32)
+        n_ct = dim // LANES
+        n_sl = -(-n_ct // n_img)
+        accc = V((2, n_chip, n_ct, rb, LANES), F32)
         dma = pltpu.SemaphoreType.DMA
         scratch = [
             feat, feat, feat, feat, feat, feat, feat, feat, V((n_blk, 3 * dim, blk), BF),
@@ -498,12 +608,16 @@
             V((2, h1, dim), F32), V((h1, dim), F32), V((n_chip, h1, dim), F32), V((2, h1, dim), F32),
             V((2, hd // 2, dim), F32), V((hd // 2, dim), F32), V((n_chip, hd // 2, dim), F32),
             V((2, hd // 2, dim), F32),
-            acc, acc, V((n_chip, n_img, rc, dim), F32), V((n_chip, n_img, rc, dim), F32),
-            V((n_off, rc, dim), F32), V((n_off, rc, dim), F32), V((n_img, rc, dim), F32), V((n_img, rc, dim), F32),
+            acc, accc, accc, V((n_chip, n_img, rc, dim), F32), V((n_chip, n_ct, rb, LANES), F32),
+            V((n_chip, n_ct, rb, LANES), F32), V((2, n_img // 2, rc, dim), F32), V((2, n_img, rc, dim), F32),
+            V((n_img - 1, rc, dim), F32), V((n_img, rc, dim), F32), V((n_sl, n_chip, n_img, rb, LANES), F32),
+            V((n_sl, n_chip, n_img, rb, LANES), F32), V((n_ct, rb, LANES), F32), V((n_ct, rb, LANES), F32),
             V((8, LANES), F32), V((8, LANES), F32), V((n_chip, n_img, 8, LANES), F32),
             dma((n_blk,)), dma((n_blk,)), dma((4,)),
             dma((n_chip + 1,)), dma((n_chip + 1,)), dma((n_chip + 1,)), dma((n_chip + 1,)),
-            dma((2,)), dma((2,)), dma((2, n_off)), dma((2, n_off)), dma((2, n_img)), dma((2, n_img)),
+            dma((3,)), dma((3,)), dma((4,)), dma((4,)), dma((n_img - 1,)), dma((n_img - 1,)),
+            dma((n_img - 1,)), dma((n_img - 1,)),
+            dma((2, n_ct, n_chip)), dma((2, n_sl, n_chip, n_img)), dma((2, n_ct, n_img - 1)), dma((2, n_ct)),
             dma((1 + n_off,)), dma((1 + n_off,)),
         ]
         out_shape = (

time: 60.7 us -> 62.5 us (1.030)
  Pallas kernels: 60 us -> 61.7 us
    pallas_call x1, Pallas kernels: 57.1 us -> 58.8 us  [local_block(): pl.pallas_call(functools.partial(_kernel, cfg), out_shape=out_shape, in_s...]
where the time goes in v3:
time: 62.5 us; the launch traced here: 62.4 us
  Pallas kernels  61.7 us (99%)
  between operations  0.64 us (1%)
    pallas_call x1, Pallas kernels, local_block(): pl.pallas_call(functools.partial(_kernel, cfg), out_shape=out_shape, in_s...  58.8 us
    pallas_call x1, Pallas kernels, local_block(): pl.pallas_call(functools.partial(_write, n_blk, blk), out_shape=finals, i...  2.88 us

profile of v3, /device:TPU:97, one launch (start us, length us, event | category | flops | bytes accessed | tf_op | source)
XLA Modules:
  0.0 62.4 jit_solution(4622436422230759857)
XLA Ops:
  0.6 58.8 %shard_map.126 = (bf16[4,1024,384]{2,1,0:T(8,128)(2,1)S(1)}, bf16[4,1024,384]{2,1,0:T(8,128)(2,1)S(1)}, f32[48,1152]{1,0:T(8,128)S(1)}, f32[48,384]{1,0:T(8,128)...) custom-call(bf16[1,4096,384]{2,1,0:T(8,128)(2,1)} %x_hbm.1, bf16[1,4096,384]{2,1,0:T(8,128)(2,1)} %gy_hbm.1, ...), custom_call_target="tpu_custom_call" | custom-call | tf_op jit(solution)/shard_map/pallas_call | solution.py:628
  59.5 2.9 %shard_map.127 = (bf16[1,4096,384]{2,1,0:T(8,128)(2,1)}, bf16[1,4096,384]{2,1,0:T(8,128)(2,1)}, f32[48,1152]{1,0:T(8,128)}, f32[48,384]{1,0:T(8,128)}, f32[384]{0:T(512)}, /*index=5*/f32[384]{0:T(512)}, f32[8]{0:T(128)}) custom-call(bf16[4,1024,384]{2,1,0:T(8,128)(2,1)S(1)} %get-tuple-element.14.refs_0_, ...), custom_call_target="tpu_custom_call" | custom-call | tf_op jit(solution)/shard_map/pallas_call | solution.py:643

commit v4 on v2

--- a/solution.py
+++ b/solution.py
@@ -36,7 +36,7 @@
 def _kernel(cfg, x_hbm, gy_hbm, gam_hbm, bet_hbm, wqkv_hbm, wout_hbm, tau_ref,
             x_v, gy_v, dwqkv_ref, dwout_ref, dgam_ref, dbet_ref, dtau_ref,
             x_t, gy_t, u_t, q_t, k_t, v_t, do_t, o_t, dqkv_t,
-            mean_v, rstd_v, w_v, w_t, wo_v, wo_t, gam_v, bet_v, gam_c, bet_c,
+            mean_v, rstd_v, k1_v, k2_v, w_v, w_t, wo_v, wo_t, gam_v, bet_v, gam_c, bet_c,
             g_lo, g_hi, da_lo, da_hi, sq_acc, sk_acc, dgam_acc, dbet_acc,
             a_f32, scale_f32, g_f32, a_lo, a_hi, at_lo, at_hi, dg_lo, dg_hi, dgt_lo, dgt_hi,
             cq_c, ck_c, srow, rqcol,
@@ -99,49 +99,81 @@
         pc, pi = peer(dc, di)
         pl.semaphore_signal(barrier, inc=1, device_id=dev(pc, core, pi), device_id_type=MESH)
 
-    for ref in (g_lo, g_hi, da_lo, da_hi, sq_acc, sk_acc, dgam_acc, dbet_acc, acc_e, acc_l):
+    spread = n_blk % n_chip == 0
+    zero = (da_lo, da_hi, dgam_acc, dbet_acc) + (() if spread else (acc_e, acc_l))
+    for ref in zero:
         ref[...] = jnp.zeros_like(ref)
 
-    loads[0].wait()
-    loads[1].wait()
+    def sub(n):
+        return slice(n * SUB, (n + 1) * SUB)
+
+    def norm(i, cols):
+        rows = 48
+        cuts = [slice(r, r + rows) for r in range(0, dim, rows)]
+
+        def fold(v):
+            t = v[0:8]
+            for r in range(8, rows, 8):
+                t += v[r:r + 8]
+            return t
+
+        s = jnp.zeros((8, LANES), F32)
+        for cut in cuts:
+            s += fold(x_t[i, cut, cols].astype(F32))
+        mean = jnp.sum(s, axis=0, keepdims=True) * inv_d
+        s = jnp.zeros((8, LANES), F32)
+        for cut in cuts:
+            cen = x_t[i, cut, cols].astype(F32) - mean
+            s += fold(cen * cen)
+        var = jnp.sum(s, axis=0, keepdims=True) * inv_d
+        rstd = lax.rsqrt(var + LN_EPS)
+        mean_v[i, :, cols] = mean
+        rstd_v[i, :, cols] = rstd
+        for cut in cuts:
+            cen = x_t[i, cut, cols].astype(F32) - mean
+            u_t[i, cut, cols] = (cen * rstd * gam_c[cut] + bet_c[cut]).astype(BF)
+
+    def norm_sub(i, n):
+        x_t[i, :, sub(n)] = jnp.transpose(x_v[i, sub(n), :])
+        for c in range(SUB // LANES):
+            norm(i, slice(n * SUB + c * LANES, n * SUB + (c + 1) * LANES))
+
+    for ld in loads:
+        ld.wait()
+    x_copy(0).wait()
     gam_c[...] = _column(gam_v[...].reshape(1, dim))
     bet_c[...] = _column(bet_v[...].reshape(1, dim))
-    loads[2].wait()
+    for n in range(n_sub):
+        norm_sub(0, n)
     for c in range(3):
         w_t[c * dim:(c + 1) * dim, :] = jnp.transpose(w_v[:, c * dim:(c + 1) * dim])
-    loads[3].wait()
     wo_t[...] = jnp.transpose(wo_v[...])
-
-    def sub(n):
-        return slice(n * SUB, (n + 1) * SUB)
-
-    def body_qk(i, _):
+    for i in range(1, n_blk):
         x_copy(i).wait()
-        for n in range(n_sub):
-            x_t[i, :, sub(n)] = jnp.transpose(x_v[i, sub(n), :])
-        for c in range(blk // LANES):
-            cols = slice(c * LANES, (c + 1) * LANES)
-            xs = x_t[i, :, cols].astype(F32)
-            mean = jnp.sum(xs, axis=0, keepdims=True) * inv_d
-            cen = xs - mean
-            var = jnp.sum(cen * cen, axis=0, keepdims=True) * inv_d
-            rstd = lax.rsqrt(var + LN_EPS)
-            mean_v[i, :, cols] = mean
-            rstd_v[i, :, cols] = rstd
-            u_t[i, :, cols] = (cen * rstd * gam_c[...] + bet_c[...]).astype(BF)
+    for i in range(n_blk):
         for n in range(n_sub):
             u_n = u_t[i, :, sub(n)]
-            for part, ref, acc in ((0, q_t, sq_acc), (1, k_t, sk_acc)):
+            for part, ref in ((0, q_t), (1, k_t)):
                 r = _dot(w_t[part * dim:(part + 1) * dim, :], u_n).astype(BF)
                 ref[i, :, sub(n)] = r
                 rf = r.astype(F32)
                 rf = rf * rf
-                acc[...] += rf[:, :LANES] + rf[:, LANES:]
-        g_lo[...] += _dot_nt(q_t[i, :r_lo, :], k_t[i, :WIN, :])
-        g_hi[...] += _dot_nt(q_t[i, r_lo:, :], k_t[i, hi0:, :])
-        return 0
-
-    lax.fori_loop(0, n_blk, body_qk, 0)
+                acc = (sq_acc, sk_acc)[part]
+                val = rf[:, :LANES] + rf[:, LANES:]
+                if i == 0 and n == 0:
+                    acc[...] = val
+                else:
+                    acc[...] += val
+            if i + 1 < n_blk:
+                norm_sub(i + 1, n)
+        lo = _dot_nt(q_t[i, :r_lo, :], k_t[i, :WIN, :])
+        hi = _dot_nt(q_t[i, r_lo:, :], k_t[i, hi0:, :])
+        if i == 0:
+            g_lo[...] = lo
+            g_hi[...] = hi
+        else:
+            g_lo[...] += lo
+            g_hi[...] += hi
 
     def pack(lo, hi, put):
         col = lax.broadcasted_iota(jnp.int32, (hd, WIN), 1)
@@ -167,7 +199,7 @@
     def ex_step2(src, rc, buf, ss, rs):
         ex_pair(src, rc, ss, rs).wait()
         buf[chip] = src[core] + rc[...]
-        for dc in range(1, n_chip):
+        for dc in sorted(range(1, n_chip), key=lambda d: -min(d, n_chip - d)):
             ex_chip(buf, ss, rs, dc).start()
 
     def ex_step3(buf, fin, ss, rs):
@@ -203,6 +235,10 @@
         for n in range(n_sub):
             v_t[i, :, sub(n)] = _dot(w_t[2 * dim:, :], u_t[i, :, sub(n)]).astype(BF)
             do_t[i, :, sub(n)] = _dot(wo_v[...], gy_t[i, :, sub(n)]).astype(BF)
+        if spread:
+            for acc in (acc_e, acc_l):
+                for p in range(2):
+                    acc[p, lax.rem(i, n_chip)] = jnp.zeros(acc.shape[2:], F32)
         da_lo[...] += _dot_nt(do_t[i, :r_lo, :], v_t[i, :WIN, :])
         da_hi[...] += _dot_nt(do_t[i, r_lo:, :], v_t[i, hi0:, :])
 
@@ -216,6 +252,7 @@
     pack(da_lo, da_hi, put_da)
     ex_pair(ex2_src, ex2_rc, ex2_ss, ex2_rs).start()
     ex_step3(ex1_x, ex1_fin, ex1_ss, ex1_rs)
+    ex_step2(ex2_src, ex2_rc, ex2_x, ex2_ss, ex2_rs)
     ex_swap(ex1_fin, ex1_ss, ex1_rs).wait()
 
     def head_mask(rows, row0, col0):
@@ -259,8 +296,6 @@
             full = jnp.concatenate([jnp.zeros((WIN - rows, WIN), F32), a], axis=0)
             a_hi[...] = full.astype(BF)
             at_hi[...] = jnp.transpose(full).astype(BF)
-
-    ex_step2(ex2_src, ex2_rc, ex2_x, ex2_ss, ex2_rs)
 
     def add_rows(acc, g, val):
         rb = dim // (2 * n_chip)
@@ -369,52 +404,64 @@
     lax.fori_loop(0, n_blk, body_qk_back, 0)
     pair_copy(1, acc_l, d2d_l).start()
 
-    def body_y(i, _):
-        for n in range(n_sub):
-            proj = _dot(wo_t[...], o_t[i, :, sub(n)])
-            x_v[i, sub(n), :] = jnp.transpose((x_t[i, :, sub(n)].astype(F32) + proj).astype(BF))
-        return 0
-
-    lax.fori_loop(0, n_blk, body_y, 0)
-    rs_start(1, acc_l, d2d_l, rs_l)
-    rs_finish(0, acc_e, rs_e, ag_e)
-
-    def body_x(i, _):
+    def body_du(i, _):
         for n in range(n_sub):
             du = _dot(w_v[...], dqkv_t[i, :, sub(n)]).astype(BF)
+            do_t[i, :, sub(n)] = du
             for c in range(SUB // LANES):
                 cols = slice(n * SUB + c * LANES, n * SUB + (c + 1) * LANES)
                 du_c = du[:, c * LANES:(c + 1) * LANES].astype(F32)
                 rstd = rstd_v[i, :, cols]
                 xh = (x_t[i, :, cols].astype(F32) - mean_v[i, :, cols]) * rstd
-                dgam_acc[...] += du_c * xh
+                p = du_c * xh
+                dgam_acc[...] += p
                 dbet_acc[...] += du_c
-                g = du_c * gam_c[...]
-                c1 = jnp.sum(g, axis=0, keepdims=True) * inv_d
-                c2 = jnp.sum(g * xh, axis=0, keepdims=True) * inv_d
-                gx = gy_t[i, :, cols].astype(F32) + rstd * (g - c1 - xh * c2)
-                gy_v[i, cols, :] = jnp.transpose(gx.astype(BF))
+                c1 = jnp.sum(du_c * gam_c[...], axis=0, keepdims=True) * inv_d
+                c2 = jnp.sum(p * gam_c[...], axis=0, keepdims=True) * inv_d
+                k1_v[i, :, cols] = rstd * c1
+                k2_v[i, :, cols] = rstd * rstd * c2
+
+        @pl.when(i == min(1, n_blk - 1))
+        def _():
+            rs_start(1, acc_l, d2d_l, rs_l)
         return 0
 
-    lax.fori_loop(0, n_blk, body_x, 0)
-
-    for b, acc in ((0, dgam_acc), (3, dbet_acc)):
+    lax.fori_loop(0, n_blk, body_du, 0)
+
+    for b, acc in ((0, dgam_acc), (dim // LANES, dbet_acc)):
         row = jnp.sum(jnp.transpose(acc[...]), axis=0, keepdims=True)
         for c in range(dim // LANES):
             gb_src[b + c:b + c + 1] = row[:, c * LANES:(c + 1) * LANES]
     gb_pair = rcopy(gb_src, gb_rc, gb_ss.at[0], gb_rs.at[0], partner)
     gb_pair.start()
 
-    gb_pair.wait()
-    gb_all[chip, img_i] = gb_src[...] + gb_rc[...]
-
     def gb_copy(n):
         pc, pi = peer(*offsets[n])
         return rcopy(gb_all.at[chip, img_i], gb_all.at[chip, img_i], gb_ss.at[1 + n], gb_rs.at[1 + n],
                      dev(pc, core, pi))
 
-    for n in range(len(offsets)):
-        gb_copy(n).start()
+    rs_finish(0, acc_e, rs_e, ag_e)
+
+    def body_x(i, _):
+        for n in range(n_sub):
+            proj = _dot(wo_t[...], o_t[i, :, sub(n)])
+            x_v[i, sub(n), :] = jnp.transpose((x_t[i, :, sub(n)].astype(F32) + proj).astype(BF))
+            for c in range(SUB // LANES):
+                cols = slice(n * SUB + c * LANES, n * SUB + (c + 1) * LANES)
+                g = do_t[i, :, cols].astype(F32) * gam_c[...] * rstd_v[i, :, cols]
+                cen = x_t[i, :, cols].astype(F32) - mean_v[i, :, cols]
+                gx = gy_t[i, :, cols].astype(F32) + (g - k1_v[i, :, cols] - cen * k2_v[i, :, cols])
+                gy_v[i, cols, :] = jnp.transpose(gx.astype(BF))
+
+        @pl.when(i == 0)
+        def _():
+            gb_pair.wait()
+            gb_all[chip, img_i] = gb_src[...] + gb_rc[...]
+            for n in range(len(offsets)):
+                gb_copy(n).start()
+        return 0
+
+    lax.fori_loop(0, n_blk, body_x, 0)
     rs_finish(1, acc_l, rs_l, ag_l)
 
     def emit(r, gbuf, outs):
@@ -488,7 +535,7 @@
         dma = pltpu.SemaphoreType.DMA
         scratch = [
             feat, feat, feat, feat, feat, feat, feat, feat, V((n_blk, 3 * dim, blk), BF),
-            stat, stat, V((dim, 3 * dim), BF), V((3 * dim, dim), BF), V((dim, dim), BF), V((dim, dim), BF),
+            stat, stat, stat, stat, V((dim, 3 * dim), BF), V((3 * dim, dim), BF), V((dim, dim), BF), V((dim, dim), BF),
             V((dim,), F32), V((dim,), F32), col, col,
             V((r_lo, WIN), F32), V((r_hi, WIN), F32), V((r_lo, WIN), F32), V((r_hi, WIN), F32),
             col, col, col, col,

time: 60.7 us -> 57.8 us (0.952)
  Pallas kernels: 60 us -> 56.6 us
    pallas_call x1, Pallas kernels: 57.1 us -> 53.7 us  [local_block(): pl.pallas_call(functools.partial(_kernel, cfg), out_shape=out_shape, in_s...]
where the time goes in v4:
time: 57.8 us; the launch traced here: 57.4 us
  Pallas kernels  56.6 us (98%)
  between operations  0.8 us (1%)
    pallas_call x1, Pallas kernels, local_block(): pl.pallas_call(functools.partial(_kernel, cfg), out_shape=out_shape, in_s...  53.7 us
    pallas_call x1, Pallas kernels, local_block(): pl.pallas_call(functools.partial(_write, n_blk, blk), out_shape=finals, i...  2.88 us

profile of v4, /device:TPU:97, one launch (start us, length us, event | category | flops | bytes accessed | tf_op | source)
XLA Modules:
  0.0 57.4 jit_solution(4144036705367547736)
XLA Ops:
  0.6 53.7 %shard_map.126 = (bf16[4,1024,384]{2,1,0:T(8,128)(2,1)S(1)}, bf16[4,1024,384]{2,1,0:T(8,128)(2,1)S(1)}, f32[48,1152]{1,0:T(8,128)S(1)}, f32[48,384]{1,0:T(8,128)...) custom-call(bf16[1,4096,384]{2,1,0:T(8,128)(2,1)} %x_hbm.1, bf16[1,4096,384]{2,1,0:T(8,128)(2,1)} %gy_hbm.1, ...), custom_call_target="tpu_custom_call" | custom-call | tf_op jit(solution)/shard_map/pallas_call | solution.py:561
  54.3 2.9 %shard_map.127 = (bf16[1,4096,384]{2,1,0:T(8,128)(2,1)}, bf16[1,4096,384]{2,1,0:T(8,128)(2,1)}, f32[48,1152]{1,0:T(8,128)}, f32[48,384]{1,0:T(8,128)}, f32[384]{0:T(512)}, /*index=5*/f32[384]{0:T(512)}, f32[8]{0:T(128)}) custom-call(bf16[4,1024,384]{2,1,0:T(8,128)(2,1)S(1)} %get-tuple-element.14.refs_0_, ...), custom_call_target="tpu_custom_call" | custom-call | tf_op jit(solution)/shard_map/pallas_call | solution.py:576

commit v5 on v3

--- a/solution.py
+++ b/solution.py
@@ -36,7 +36,7 @@
 def _kernel(cfg, x_hbm, gy_hbm, gam_hbm, bet_hbm, wqkv_hbm, wout_hbm, tau_ref,
             x_v, gy_v, dwqkv_ref, dwout_ref, dgam_ref, dbet_ref, dtau_ref,
             x_t, gy_t, u_t, q_t, k_t, v_t, do_t, o_t, dqkv_t,
-            mean_v, rstd_v, w_v, w_t, wo_v, wo_t, gam_v, bet_v, gam_c, bet_c,
+            mean_v, rstd_v, k1_v, k2_v, w_v, w_t, wo_v, wo_t, gam_v, bet_v, gam_c, bet_c,
             g_lo, g_hi, da_lo, da_hi, sq_acc, sk_acc, dgam_acc, dbet_acc,
             a_f32, scale_f32, g_f32, a_lo, a_hi, at_lo, at_hi, dg_lo, dg_hi, dgt_lo, dgt_hi,
             cq_c, ck_c, srow, rqcol,
@@ -100,49 +100,81 @@
         pc, pi = peer(dc, di)
         pl.semaphore_signal(barrier, inc=1, device_id=dev(pc, core, pi), device_id_type=MESH)
 
-    for ref in (g_lo, g_hi, da_lo, da_hi, sq_acc, sk_acc, dgam_acc, dbet_acc, acc_e, acc_q, acc_k):
+    spread = n_blk % n_chip == 0
+    zero = (da_lo, da_hi, dgam_acc, dbet_acc) + (() if spread else (acc_e,))
+    for ref in zero:
         ref[...] = jnp.zeros_like(ref)
 
-    loads[0].wait()
-    loads[1].wait()
+    def sub(n):
+        return slice(n * SUB, (n + 1) * SUB)
+
+    def norm(i, cols):
+        rows = 48
+        cuts = [slice(r, r + rows) for r in range(0, dim, rows)]
+
+        def fold(v):
+            t = v[0:8]
+            for r in range(8, rows, 8):
+                t += v[r:r + 8]
+            return t
+
+        s = jnp.zeros((8, LANES), F32)
+        for cut in cuts:
+            s += fold(x_t[i, cut, cols].astype(F32))
+        mean = jnp.sum(s, axis=0, keepdims=True) * inv_d
+        s = jnp.zeros((8, LANES), F32)
+        for cut in cuts:
+            cen = x_t[i, cut, cols].astype(F32) - mean
+            s += fold(cen * cen)
+        var = jnp.sum(s, axis=0, keepdims=True) * inv_d
+        rstd = lax.rsqrt(var + LN_EPS)
+        mean_v[i, :, cols] = mean
+        rstd_v[i, :, cols] = rstd
+        for cut in cuts:
+            cen = x_t[i, cut, cols].astype(F32) - mean
+            u_t[i, cut, cols] = (cen * rstd * gam_c[cut] + bet_c[cut]).astype(BF)
+
+    def norm_sub(i, n):
+        x_t[i, :, sub(n)] = jnp.transpose(x_v[i, sub(n), :])
+        for c in range(SUB // LANES):
+            norm(i, slice(n * SUB + c * LANES, n * SUB + (c + 1) * LANES))
+
+    for ld in loads:
+        ld.wait()
+    x_copy(0).wait()
     gam_c[...] = _column(gam_v[...].reshape(1, dim))
     bet_c[...] = _column(bet_v[...].reshape(1, dim))
-    loads[2].wait()
+    for n in range(n_sub):
+        norm_sub(0, n)
     for c in range(3):
         w_t[c * dim:(c + 1) * dim, :] = jnp.transpose(w_v[:, c * dim:(c + 1) * dim])
-    loads[3].wait()
     wo_t[...] = jnp.transpose(wo_v[...])
-
-    def sub(n):
-        return slice(n * SUB, (n + 1) * SUB)
-
-    def body_qk(i, _):
+    for i in range(1, n_blk):
         x_copy(i).wait()
-        for n in range(n_sub):
-            x_t[i, :, sub(n)] = jnp.transpose(x_v[i, sub(n), :])
-        for c in range(blk // LANES):
-            cols = slice(c * LANES, (c + 1) * LANES)
-            xs = x_t[i, :, cols].astype(F32)
-            mean = jnp.sum(xs, axis=0, keepdims=True) * inv_d
-            cen = xs - mean
-            var = jnp.sum(cen * cen, axis=0, keepdims=True) * inv_d
-            rstd = lax.rsqrt(var + LN_EPS)
-            mean_v[i, :, cols] = mean
-            rstd_v[i, :, cols] = rstd
-            u_t[i, :, cols] = (cen * rstd * gam_c[...] + bet_c[...]).astype(BF)
+    for i in range(n_blk):
         for n in range(n_sub):
             u_n = u_t[i, :, sub(n)]
-            for part, ref, acc in ((0, q_t, sq_acc), (1, k_t, sk_acc)):
+            for part, ref in ((0, q_t), (1, k_t)):
                 r = _dot(w_t[part * dim:(part + 1) * dim, :], u_n).astype(BF)
                 ref[i, :, sub(n)] = r
                 rf = r.astype(F32)
                 rf = rf * rf
-                acc[...] += rf[:, :LANES] + rf[:, LANES:]
-        g_lo[...] += _dot_nt(q_t[i, :r_lo, :], k_t[i, :WIN, :])
-        g_hi[...] += _dot_nt(q_t[i, r_lo:, :], k_t[i, hi0:, :])
-        return 0
-
-    lax.fori_loop(0, n_blk, body_qk, 0)
+                acc = (sq_acc, sk_acc)[part]
+                val = rf[:, :LANES] + rf[:, LANES:]
+                if i == 0 and n == 0:
+                    acc[...] = val
+                else:
+                    acc[...] += val
+            if i + 1 < n_blk:
+                norm_sub(i + 1, n)
+        lo = _dot_nt(q_t[i, :r_lo, :], k_t[i, :WIN, :])
+        hi = _dot_nt(q_t[i, r_lo:, :], k_t[i, hi0:, :])
+        if i == 0:
+            g_lo[...] = lo
+            g_hi[...] = hi
+        else:
+            g_lo[...] += lo
+            g_hi[...] += hi
 
     def pack(lo, hi, put):
         col = lax.broadcasted_iota(jnp.int32, (hd, WIN), 1)
@@ -168,7 +200,7 @@
     def ex_step2(src, rc, buf, ss, rs):
         ex_pair(src, rc, ss, rs).wait()
         buf[chip] = src[core] + rc[...]
-        for dc in range(1, n_chip):
+        for dc in sorted(range(1, n_chip), key=lambda d: -min(d, n_chip - d)):
             ex_chip(buf, ss, rs, dc).start()
 
     def ex_step3(buf, fin, ss, rs):
@@ -204,6 +236,9 @@
         for n in range(n_sub):
             v_t[i, :, sub(n)] = _dot(w_t[2 * dim:, :], u_t[i, :, sub(n)]).astype(BF)
             do_t[i, :, sub(n)] = _dot(wo_v[...], gy_t[i, :, sub(n)]).astype(BF)
+        if spread:
+            for p in range(2):
+                acc_e[p, lax.rem(i, n_chip)] = jnp.zeros(acc_e.shape[2:], F32)
         da_lo[...] += _dot_nt(do_t[i, :r_lo, :], v_t[i, :WIN, :])
         da_hi[...] += _dot_nt(do_t[i, r_lo:, :], v_t[i, hi0:, :])
 
@@ -217,6 +252,7 @@
     pack(da_lo, da_hi, put_da)
     ex_pair(ex2_src, ex2_rc, ex2_ss, ex2_rs).start()
     ex_step3(ex1_x, ex1_fin, ex1_ss, ex1_rs)
+    ex_step2(ex2_src, ex2_rc, ex2_x, ex2_ss, ex2_rs)
     ex_swap(ex1_fin, ex1_ss, ex1_rs).wait()
 
     def head_mask(rows, row0, col0):
@@ -261,8 +297,6 @@
             a_hi[...] = full.astype(BF)
             at_hi[...] = jnp.transpose(full).astype(BF)
 
-    ex_step2(ex2_src, ex2_rc, ex2_x, ex2_ss, ex2_rs)
-
     def add_rows(acc, g, val):
         rb = dim // (2 * n_chip)
         n_a = n_img // 2
@@ -273,11 +307,15 @@
 
     n_ct = dim // LANES
 
-    def add_cols(acc, val):
+    def add_cols(acc, val, first):
         rb = dim // (2 * n_chip)
         for s in range(2 * n_chip):
             for ct in range(n_ct):
-                acc[s % 2, s // 2, ct] += val[s * rb:(s + 1) * rb, ct * LANES:(ct + 1) * LANES]
+                part = val[s * rb:(s + 1) * rb, ct * LANES:(ct + 1) * LANES]
+                if first:
+                    acc[s % 2, s // 2, ct] = part
+                else:
+                    acc[s % 2, s // 2, ct] += part
 
     def body_ov(i, _):
         for n in range(n_sub):
@@ -287,6 +325,10 @@
             dqkv_t[i, 2 * dim + r_lo:, sub(n)] = _dot(at_hi[off_hi:], do_t[i, hi0:, sub(n)]).astype(BF)
         add_rows(acc_e, 0, _dot(o_t[i], gy_v[i]))
         add_rows(acc_e, 1, _dot_nt(u_t[i], dqkv_t[i, 2 * dim:, :]))
+
+        @pl.when(i == max(n_blk - 2, 0))
+        def _():
+            ex_step3(ex2_x, ex2_fin, ex2_ss, ex2_rs)
         return 0
 
     lax.fori_loop(0, n_blk, body_ov, 0)
@@ -406,7 +448,6 @@
                 ag_copy(r, gbuf, ct, 1).wait_recv()
             ref[:, col + ct * LANES:col + (ct + 1) * LANES] = gbuf[ct]
 
-    ex_step3(ex2_x, ex2_fin, ex2_ss, ex2_rs)
     pair_copy(0, acc_e, d2d_e).start()
     ex_swap(ex2_fin, ex2_ss, ex2_rs).wait()
 
@@ -448,84 +489,94 @@
     gb_src[6:7] = jnp.where(seq_i == 0, dtau_row, 0.0)
     gb_src[7:8] = jnp.zeros((1, LANES), F32)
 
+    def back(i, part):
+        lo, hi, a_t, b_t, c = ((dg_lo, dg_hi, k_t, q_t, cq_c), (dgt_lo, dgt_hi, q_t, k_t, ck_c))[part]
+        base = part * dim
+        for n in range(n_sub):
+            a_n = a_t[i, :, sub(n)]
+            d = jnp.concatenate([_dot(lo[:r_lo], a_n[:WIN]), _dot(hi[off_hi:], a_n[hi0:])], axis=0)
+            dqkv_t[i, base:base + dim, sub(n)] = (d + _twice(c[...]) * b_t[i, :, sub(n)].astype(F32)).astype(BF)
+        add_cols((acc_q, acc_k)[part], _dot_nt(u_t[i], dqkv_t[i, base:base + dim, :]), i == 0)
+
+    back(0, 0)
     e_step1()
-
-    def body_qk_back(i, _):
-        for n in range(n_sub):
-            k_n = k_t[i, :, sub(n)]
-            q_n = q_t[i, :, sub(n)]
-            dq = jnp.concatenate([_dot(dg_lo[:r_lo], k_n[:WIN]), _dot(dg_hi[off_hi:], k_n[hi0:])], axis=0)
-            dqkv_t[i, :dim, sub(n)] = (dq + _twice(cq_c[...]) * q_n.astype(F32)).astype(BF)
-            dk = jnp.concatenate([_dot(dgt_lo[:r_lo], q_n[:WIN]), _dot(dgt_hi[off_hi:], q_n[hi0:])], axis=0)
-            dqkv_t[i, dim:2 * dim, sub(n)] = (dk + _twice(ck_c[...]) * k_n.astype(F32)).astype(BF)
-        add_cols(acc_q, _dot_nt(u_t[i], dqkv_t[i, :dim, :]))
-        return 0
-
-    lax.fori_loop(0, n_blk, body_qk_back, 0)
+    for i in range(1, n_blk):
+        back(i, 0)
     pair_copy(1, acc_q, d2d_q).start()
-    e_step2()
-
-    def body_wk(i, _):
-        add_cols(acc_k, _dot_nt(u_t[i], dqkv_t[i, dim:2 * dim, :]))
-        return 0
-
-    lax.fori_loop(0, n_blk, body_wk, 0)
+    for i in range(n_blk):
+        back(i, 1)
+        if i == min(1, n_blk - 1):
+            rs_start(0, acc_q, d2d_q, rs_q)
+            e_step2()
     pair_copy(2, acc_k, d2d_k).start()
-    rs_start(0, acc_q, d2d_q, rs_q)
-
-    def body_y(i, _):
-        for n in range(n_sub):
-            proj = _dot(wo_t[...], o_t[i, :, sub(n)])
-            x_v[i, sub(n), :] = jnp.transpose((x_t[i, :, sub(n)].astype(F32) + proj).astype(BF))
-        return 0
-
-    lax.fori_loop(0, n_blk, body_y, 0)
-    rs_start(1, acc_k, d2d_k, rs_k)
-
-    def body_x(i, _):
+
+    def body_du(i, _):
         for n in range(n_sub):
             du = _dot(w_v[...], dqkv_t[i, :, sub(n)]).astype(BF)
+            do_t[i, :, sub(n)] = du
             for c in range(SUB // LANES):
                 cols = slice(n * SUB + c * LANES, n * SUB + (c + 1) * LANES)
                 du_c = du[:, c * LANES:(c + 1) * LANES].astype(F32)
                 rstd = rstd_v[i, :, cols]
                 xh = (x_t[i, :, cols].astype(F32) - mean_v[i, :, cols]) * rstd
-                dgam_acc[...] += du_c * xh
+                p = du_c * xh
+                dgam_acc[...] += p
                 dbet_acc[...] += du_c
-                g = du_c * gam_c[...]
-                c1 = jnp.sum(g, axis=0, keepdims=True) * inv_d
-                c2 = jnp.sum(g * xh, axis=0, keepdims=True) * inv_d
-                gx = gy_t[i, :, cols].astype(F32) + rstd * (g - c1 - xh * c2)
-                gy_v[i, cols, :] = jnp.transpose(gx.astype(BF))
+                c1 = jnp.sum(du_c * gam_c[...], axis=0, keepdims=True) * inv_d
+                c2 = jnp.sum(p * gam_c[...], axis=0, keepdims=True) * inv_d
+                k1_v[i, :, cols] = rstd * c1
+                k2_v[i, :, cols] = rstd * rstd * c2
 
         @pl.when(i == 0)
+        def _():
+            rs_start(1, acc_k, d2d_k, rs_k)
+
+        @pl.when(i == min(2, n_blk - 1))
         def _():
             e_step3()
         return 0
 
-    lax.fori_loop(0, n_blk, body_x, 0)
-
-    for b, acc in ((0, dgam_acc), (3, dbet_acc)):
+    lax.fori_loop(0, n_blk, body_du, 0)
+
+    for b, acc in ((0, dgam_acc), (dim // LANES, dbet_acc)):
         row = jnp.sum(jnp.transpose(acc[...]), axis=0, keepdims=True)
         for c in range(dim // LANES):
             gb_src[b + c:b + c + 1] = row[:, c * LANES:(c + 1) * LANES]
     gb_pair = rcopy(gb_src, gb_rc, gb_ss.at[0], gb_rs.at[0], partner)
     gb_pair.start()
 
-    gb_pair.wait()
-    gb_all[chip, img_i] = gb_src[...] + gb_rc[...]
-
     def gb_copy(n):
         pc, pi = peer(*offsets[n])
         return rcopy(gb_all.at[chip, img_i], gb_all.at[chip, img_i], gb_ss.at[1 + n], gb_rs.at[1 + n],
                      dev(pc, core, pi))
 
-    for n in range(len(offsets)):
-        gb_copy(n).start()
     rs_finish(0, acc_q, rs_q, ag_q)
-    e_step4()
-    rs_finish(1, acc_k, rs_k, ag_k)
-
+
+    def body_x(i, _):
+        for n in range(n_sub):
+            proj = _dot(wo_t[...], o_t[i, :, sub(n)])
+            x_v[i, sub(n), :] = jnp.transpose((x_t[i, :, sub(n)].astype(F32) + proj).astype(BF))
+            for c in range(SUB // LANES):
+                cols = slice(n * SUB + c * LANES, n * SUB + (c + 1) * LANES)
+                g = do_t[i, :, cols].astype(F32) * gam_c[...] * rstd_v[i, :, cols]
+                cen = x_t[i, :, cols].astype(F32) - mean_v[i, :, cols]
+                gx = gy_t[i, :, cols].astype(F32) + (g - k1_v[i, :, cols] - cen * k2_v[i, :, cols])
+                gy_v[i, cols, :] = jnp.transpose(gx.astype(BF))
+
+        @pl.when(i == 0)
+        def _():
+            gb_pair.wait()
+            gb_all[chip, img_i] = gb_src[...] + gb_rc[...]
+            for n in range(len(offsets)):
+                gb_copy(n).start()
+            e_step4()
+
+        @pl.when(i == max(n_blk - 2, 0))
+        def _():
+            rs_finish(1, acc_k, rs_k, ag_k)
+        return 0
+
+    lax.fori_loop(0, n_blk, body_x, 0)
     for n in range(len(offsets)):
         gb_copy(n).wait()
     tot = jnp.zeros(gb_src.shape, F32)
@@ -598,7 +649,7 @@
         dma = pltpu.SemaphoreType.DMA
         scratch = [
             feat, feat, feat, feat, feat, feat, feat, feat, V((n_blk, 3 * dim, blk), BF),
-            stat, stat, V((dim, 3 * dim), BF), V((3 * dim, dim), BF), V((dim, dim), BF), V((dim, dim), BF),
+            stat, stat, stat, stat, V((dim, 3 * dim), BF), V((3 * dim, dim), BF), V((dim, dim), BF), V((dim, dim), BF),
             V((dim,), F32), V((dim,), F32), col, col,
             V((r_lo, WIN), F32), V((r_hi, WIN), F32), V((r_lo, WIN), F32), V((r_hi, WIN), F32),
             col, col, col, col,

time: 62.5 us -> 57.7 us (0.923)
  Pallas kernels: 61.7 us -> 56.8 us
    pallas_call x1, Pallas kernels: 58.8 us -> 53.9 us  [local_block(): pl.pallas_call(functools.partial(_kernel, cfg), out_shape=out_shape, in_s...]
where the time goes in v5:
time: 57.7 us; the launch traced here: 57.6 us
  Pallas kernels  56.8 us (98%)
  between operations  0.8 us (1%)
    pallas_call x1, Pallas kernels, local_block(): pl.pallas_call(functools.partial(_kernel, cfg), out_shape=out_shape, in_s...  53.9 us
    pallas_call x1, Pallas kernels, local_block(): pl.pallas_call(functools.partial(_write, n_blk, blk), out_shape=finals, i...  2.88 us

profile of v5, /device:TPU:97, one launch (start us, length us, event | category | flops | bytes accessed | tf_op | source)
XLA Modules:
  0.0 57.6 jit_solution(1939664762892951899)
XLA Ops:
  0.6 53.9 %shard_map.126 = (bf16[4,1024,384]{2,1,0:T(8,128)(2,1)S(1)}, bf16[4,1024,384]{2,1,0:T(8,128)(2,1)S(1)}, f32[48,1152]{1,0:T(8,128)S(1)}, f32[48,384]{1,0:T(8,128)...) custom-call(bf16[1,4096,384]{2,1,0:T(8,128)(2,1)} %x_hbm.1, bf16[1,4096,384]{2,1,0:T(8,128)(2,1)} %gy_hbm.1, ...), custom_call_target="tpu_custom_call" | custom-call | tf_op jit(solution)/shard_map/pallas_call | solution.py:679
  54.6 2.9 %shard_map.127 = (bf16[1,4096,384]{2,1,0:T(8,128)(2,1)}, bf16[1,4096,384]{2,1,0:T(8,128)(2,1)}, f32[48,1152]{1,0:T(8,128)}, f32[48,384]{1,0:T(8,128)}, f32[384]{0:T(512)}, /*index=5*/f32[384]{0:T(512)}, f32[8]{0:T(128)}) custom-call(bf16[4,1024,384]{2,1,0:T(8,128)(2,1)S(1)} %get-tuple-element.14.refs_0_, ...), custom_call_target="tpu_custom_call" | custom-call | tf_op jit(solution)/shard_map/pallas_call | solution.py:694

commit v6 on v5

--- a/solution.py
+++ b/solution.py
@@ -88,11 +88,7 @@
     loads[1].start()
     x_copy(0).start()
     loads[2].start()
-    for i in range(1, n_blk):
-        x_copy(i).start()
     loads[3].start()
-    for i in range(n_blk):
-        gy_copy(i).start()
 
     barrier = pltpu.get_barrier_semaphore()
     pl.semaphore_signal(barrier, inc=1, device_id=partner, device_id_type=MESH)
@@ -100,8 +96,10 @@
         pc, pi = peer(dc, di)
         pl.semaphore_signal(barrier, inc=1, device_id=dev(pc, core, pi), device_id_type=MESH)
 
-    spread = n_blk % n_chip == 0
-    zero = (da_lo, da_hi, dgam_acc, dbet_acc) + (() if spread else (acc_e,))
+    for i in range(1, n_blk):
+        x_copy(i).start()
+
+    zero = (dgam_acc, dbet_acc)
     for ref in zero:
         ref[...] = jnp.zeros_like(ref)
 
@@ -151,6 +149,8 @@
     wo_t[...] = jnp.transpose(wo_v[...])
     for i in range(1, n_blk):
         x_copy(i).wait()
+    for i in range(n_blk):
+        gy_copy(i).start()
     for i in range(n_blk):
         for n in range(n_sub):
             u_n = u_t[i, :, sub(n)]
@@ -229,25 +229,22 @@
     pl.semaphore_wait(barrier, 1 + len(offsets))
     ex_pair(ex1_src, ex1_rc, ex1_ss, ex1_rs).start()
 
-    def body_v(i, _):
+    for i in range(n_blk):
         gy_copy(i).wait()
+    for i in range(n_blk):
         for n in range(n_sub):
             gy_t[i, :, sub(n)] = jnp.transpose(gy_v[i, sub(n), :])
-        for n in range(n_sub):
             v_t[i, :, sub(n)] = _dot(w_t[2 * dim:, :], u_t[i, :, sub(n)]).astype(BF)
             do_t[i, :, sub(n)] = _dot(wo_v[...], gy_t[i, :, sub(n)]).astype(BF)
-        if spread:
-            for p in range(2):
-                acc_e[p, lax.rem(i, n_chip)] = jnp.zeros(acc_e.shape[2:], F32)
-        da_lo[...] += _dot_nt(do_t[i, :r_lo, :], v_t[i, :WIN, :])
-        da_hi[...] += _dot_nt(do_t[i, r_lo:, :], v_t[i, hi0:, :])
-
-        @pl.when(i == 0)
-        def _():
+        lo = _dot_nt(do_t[i, :r_lo, :], v_t[i, :WIN, :])
+        hi = _dot_nt(do_t[i, r_lo:, :], v_t[i, hi0:, :])
+        if i == 0:
+            da_lo[...] = lo
+            da_hi[...] = hi
             ex_step2(ex1_src, ex1_rc, ex1_x, ex1_ss, ex1_rs)
-        return 0
-
-    lax.fori_loop(0, n_blk, body_v, 0)
+        else:
+            da_lo[...] += lo
+            da_hi[...] += hi
 
     pack(da_lo, da_hi, put_da)
     ex_pair(ex2_src, ex2_rc, ex2_ss, ex2_rs).start()
@@ -297,13 +294,17 @@
             a_hi[...] = full.astype(BF)
             at_hi[...] = jnp.transpose(full).astype(BF)
 
-    def add_rows(acc, g, val):
+    def add_rows(acc, g, val, first):
         rb = dim // (2 * n_chip)
         n_a = n_img // 2
         rc = rb // n_a
         for s in range(2 * n_chip):
             for a in range(n_a):
-                acc[s % 2, s // 2, 2 * a + g] += val[s * rb + a * rc:s * rb + (a + 1) * rc]
+                part = val[s * rb + a * rc:s * rb + (a + 1) * rc]
+                if first:
+                    acc[s % 2, s // 2, 2 * a + g] = part
+                else:
+                    acc[s % 2, s // 2, 2 * a + g] += part
 
     n_ct = dim // LANES
 
@@ -317,21 +318,16 @@
                 else:
                     acc[s % 2, s // 2, ct] += part
 
-    def body_ov(i, _):
+    for i in range(n_blk):
         for n in range(n_sub):
             o_t[i, :r_lo, sub(n)] = _dot(a_lo[:r_lo], v_t[i, :WIN, sub(n)]).astype(BF)
             o_t[i, r_lo:, sub(n)] = _dot(a_hi[off_hi:], v_t[i, hi0:, sub(n)]).astype(BF)
             dqkv_t[i, 2 * dim:2 * dim + r_lo, sub(n)] = _dot(at_lo[:r_lo], do_t[i, :WIN, sub(n)]).astype(BF)
             dqkv_t[i, 2 * dim + r_lo:, sub(n)] = _dot(at_hi[off_hi:], do_t[i, hi0:, sub(n)]).astype(BF)
-        add_rows(acc_e, 0, _dot(o_t[i], gy_v[i]))
-        add_rows(acc_e, 1, _dot_nt(u_t[i], dqkv_t[i, 2 * dim:, :]))
-
-        @pl.when(i == max(n_blk - 2, 0))
-        def _():
+        add_rows(acc_e, 0, _dot(o_t[i], gy_v[i]), i == 0)
+        add_rows(acc_e, 1, _dot_nt(u_t[i], dqkv_t[i, 2 * dim:, :]), i == 0)
+        if i == max(n_blk - 2, 0):
             ex_step3(ex2_x, ex2_fin, ex2_ss, ex2_rs)
-        return 0
-
-    lax.fori_loop(0, n_blk, body_ov, 0)
 
     def pair_copy(r, acc, buf):
         return rcopy(acc.at[1 - core], buf, d2d_ss.at[r], d2d_rs.at[r], partner)
@@ -498,16 +494,15 @@
             dqkv_t[i, base:base + dim, sub(n)] = (d + _twice(c[...]) * b_t[i, :, sub(n)].astype(F32)).astype(BF)
         add_cols((acc_q, acc_k)[part], _dot_nt(u_t[i], dqkv_t[i, base:base + dim, :]), i == 0)
 
-    back(0, 0)
     e_step1()
-    for i in range(1, n_blk):
+    for i in range(n_blk):
         back(i, 0)
     pair_copy(1, acc_q, d2d_q).start()
+    e_step2()
     for i in range(n_blk):
         back(i, 1)
         if i == min(1, n_blk - 1):
             rs_start(0, acc_q, d2d_q, rs_q)
-            e_step2()
     pair_copy(2, acc_k, d2d_k).start()
 
     def body_du(i, _):
@@ -531,7 +526,7 @@
         def _():
             rs_start(1, acc_k, d2d_k, rs_k)
 
-        @pl.when(i == min(2, n_blk - 1))
+        @pl.when(i == min(1, n_blk - 1))
         def _():
             e_step3()
         return 0
@@ -550,7 +545,6 @@
         return rcopy(gb_all.at[chip, img_i], gb_all.at[chip, img_i], gb_ss.at[1 + n], gb_rs.at[1 + n],
                      dev(pc, core, pi))
 
-    rs_finish(0, acc_q, rs_q, ag_q)
 
     def body_x(i, _):
         for n in range(n_sub):
@@ -569,14 +563,15 @@
             gb_all[chip, img_i] = gb_src[...] + gb_rc[...]
             for n in range(len(offsets)):
                 gb_copy(n).start()
+            rs_finish(0, acc_q, rs_q, ag_q)
+
+        @pl.when(i == min(1, n_blk - 1))
+        def _():
             e_step4()
-
-        @pl.when(i == max(n_blk - 2, 0))
-        def _():
-            rs_finish(1, acc_k, rs_k, ag_k)
         return 0
 
     lax.fori_loop(0, n_blk, body_x, 0)
+    rs_finish(1, acc_k, rs_k, ag_k)
     for n in range(len(offsets)):
         gb_copy(n).wait()
     tot = jnp.zeros(gb_src.shape, F32)

time: 57.7 us -> 56.3 us (0.976)
  Pallas kernels: 56.8 us -> 55.3 us
    pallas_call x1, Pallas kernels: 53.9 us -> 52.5 us  [local_block(): pl.pallas_call(functools.partial(_kernel, cfg), out_shape=out_shape, in_s...]
where the time goes in v6:
time: 56.3 us; the launch traced here: 56.2 us
  Pallas kernels  55.3 us (98%)
  between operations  0.82 us (1%)
    pallas_call x1, Pallas kernels, local_block(): pl.pallas_call(functools.partial(_kernel, cfg), out_shape=out_shape, in_s...  52.5 us
    pallas_call x1, Pallas kernels, local_block(): pl.pallas_call(functools.partial(_write, n_blk, blk), out_shape=finals, i...  2.88 us

profile of v6, /device:TPU:97, one launch (start us, length us, event | category | flops | bytes accessed | tf_op | source)
XLA Modules:
  0.0 56.2 jit_solution(3938164098416849981)
XLA Ops:
  0.6 52.5 %shard_map.126 = (bf16[4,1024,384]{2,1,0:T(8,128)(2,1)S(1)}, bf16[4,1024,384]{2,1,0:T(8,128)(2,1)S(1)}, f32[48,1152]{1,0:T(8,128)S(1)}, f32[48,384]{1,0:T(8,128)...) custom-call(bf16[1,4096,384]{2,1,0:T(8,128)(2,1)} %x_hbm.1, bf16[1,4096,384]{2,1,0:T(8,128)(2,1)} %gy_hbm.1, ...), custom_call_target="tpu_custom_call" | custom-call | tf_op jit(solution)/shard_map/pallas_call | solution.py:674
  53.1 2.9 %shard_map.127 = (bf16[1,4096,384]{2,1,0:T(8,128)(2,1)}, bf16[1,4096,384]{2,1,0:T(8,128)(2,1)}, f32[48,1152]{1,0:T(8,128)}, f32[48,384]{1,0:T(8,128)}, f32[384]{0:T(512)}, /*index=5*/f32[384]{0:T(512)}, f32[8]{0:T(128)}) custom-call(bf16[4,1024,384]{2,1,0:T(8,128)(2,1)S(1)} %get-tuple-element.14.refs_0_, ...), custom_call_target="tpu_custom_call" | custom-call | tf_op jit(solution)/shard_map/pallas_call | solution.py:689

commit v7 on v6

--- a/solution.py
+++ b/solution.py
@@ -333,6 +333,7 @@
         return rcopy(acc.at[1 - core], buf, d2d_ss.at[r], d2d_rs.at[r], partner)
 
     hn = n_img // 2
+    far_first = sorted(range(1, n_img), key=lambda d: -min(d, n_img - d))
     right = lax.rem(chip + 1, n_chip)
     left = lax.rem(chip + n_chip - 1, n_chip)
     opp = lax.rem(chip + 2, n_chip)
@@ -375,7 +376,7 @@
         ring_copy(2).wait()
         ring_copy(3).wait()
         acc_e[core, chip] += ring2[0] + ring2[1]
-        for di in range(1, n_img):
+        for di in far_first:
             yrs_copy(di).start()
 
     def e_step4():
@@ -384,7 +385,7 @@
             yrs_copy(di).wait()
             tot += yrs_e[di - 1]
         ag_e[img_i] = tot
-        for di in range(1, n_img):
+        for di in far_first:
             age_copy(di).start()
 
     def owner(r, ct):
@@ -397,7 +398,7 @@
                      dev(pc, core, owner(r, ct)))
 
     def each_send(r, do):
-        for dc in range(n_chip):
+        for dc in sorted(range(n_chip), key=lambda d: -min(d, n_chip - d)):
             for ct in range(n_ct):
                 if dc:
                     do(ct, dc)
@@ -428,7 +429,7 @@
                               partner).wait_recv()
                         tot += buf[sl, dc, im]
                 gbuf[ct] = tot
-                for di in range(1, n_img):
+                for di in far_first:
                     ag_copy(r, gbuf, ct, di).start()
 
     def rs_end(r, acc, buf, gbuf, ref, col):
@@ -497,11 +498,12 @@
     e_step1()
     for i in range(n_blk):
         back(i, 0)
+        if i == max(n_blk - 2, 0):
+            e_step2()
     pair_copy(1, acc_q, d2d_q).start()
-    e_step2()
     for i in range(n_blk):
         back(i, 1)
-        if i == min(1, n_blk - 1):
+        if i == 0:
             rs_start(0, acc_q, d2d_q, rs_q)
     pair_copy(2, acc_k, d2d_k).start()
 
@@ -568,10 +570,13 @@
         @pl.when(i == min(1, n_blk - 1))
         def _():
             e_step4()
+
+        @pl.when(i == max(n_blk - 2, 0))
+        def _():
+            rs_finish(1, acc_k, rs_k, ag_k)
         return 0
 
     lax.fori_loop(0, n_blk, body_x, 0)
-    rs_finish(1, acc_k, rs_k, ag_k)
     for n in range(len(offsets)):
         gb_copy(n).wait()
     tot = jnp.zeros(gb_src.shape, F32)

time: 56.3 us -> 57.1 us (1.014)
  Pallas kernels: 55.3 us -> 56.2 us
    pallas_call x1, Pallas kernels: 52.5 us -> 53.3 us  [local_block(): pl.pallas_call(functools.partial(_kernel, cfg), out_shape=out_shape, in_s...]
where the time goes in v7:
time: 57.1 us; the launch traced here: 57 us
  Pallas kernels  56.2 us (98%)
  between operations  0.82 us (1%)
    pallas_call x1, Pallas kernels, local_block(): pl.pallas_call(functools.partial(_kernel, cfg), out_shape=out_shape, in_s...  53.3 us
    pallas_call x1, Pallas kernels, local_block(): pl.pallas_call(functools.partial(_write, n_blk, blk), out_shape=finals, i...  2.88 us

profile of v7, /device:TPU:97, one launch (start us, length us, event | category | flops | bytes accessed | tf_op | source)
XLA Modules:
  0.0 57.0 jit_solution(14706808798401321767)
XLA Ops:
  0.6 53.3 %shard_map.126 = (bf16[4,1024,384]{2,1,0:T(8,128)(2,1)S(1)}, bf16[4,1024,384]{2,1,0:T(8,128)(2,1)S(1)}, f32[48,1152]{1,0:T(8,128)S(1)}, f32[48,384]{1,0:T(8,128)...) custom-call(bf16[1,4096,384]{2,1,0:T(8,128)(2,1)} %x_hbm.1, bf16[1,4096,384]{2,1,0:T(8,128)(2,1)} %gy_hbm.1, ...), custom_call_target="tpu_custom_call" | custom-call | tf_op jit(solution)/shard_map/pallas_call | solution.py:679
  53.9 2.9 %shard_map.127 = (bf16[1,4096,384]{2,1,0:T(8,128)(2,1)}, bf16[1,4096,384]{2,1,0:T(8,128)(2,1)}, f32[48,1152]{1,0:T(8,128)}, f32[48,384]{1,0:T(8,128)}, f32[384]{0:T(512)}, /*index=5*/f32[384]{0:T(512)}, f32[8]{0:T(128)}) custom-call(bf16[4,1024,384]{2,1,0:T(8,128)(2,1)S(1)} %get-tuple-element.14.refs_0_, ...), custom_call_target="tpu_custom_call" | custom-call | tf_op jit(solution)/shard_map/pallas_call | solution.py:694

commit v8 on v6

--- a/solution.py
+++ b/solution.py
@@ -505,7 +505,7 @@
             rs_start(0, acc_q, d2d_q, rs_q)
     pair_copy(2, acc_k, d2d_k).start()
 
-    def body_du(i, _):
+    for i in range(n_blk):
         for n in range(n_sub):
             du = _dot(w_v[...], dqkv_t[i, :, sub(n)]).astype(BF)
             do_t[i, :, sub(n)] = du
@@ -522,16 +522,10 @@
                 k1_v[i, :, cols] = rstd * c1
                 k2_v[i, :, cols] = rstd * rstd * c2
 
-        @pl.when(i == 0)
-        def _():
+        if i == 0:
             rs_start(1, acc_k, d2d_k, rs_k)
-
-        @pl.when(i == min(1, n_blk - 1))
-        def _():
+        if i == min(1, n_blk - 1):
             e_step3()
-        return 0
-
-    lax.fori_loop(0, n_blk, body_du, 0)
 
     for b, acc in ((0, dgam_acc), (dim // LANES, dbet_acc)):
         row = jnp.sum(jnp.transpose(acc[...]), axis=0, keepdims=True)

time: 56.3 us -> 56.2 us (level)
  no operation moved by 1% of the time
where the time goes in v8:
time: 56.2 us; the launch traced here: 56.1 us
  Pallas kernels  55.3 us (98%)
  between operations  0.82 us (1%)
    pallas_call x1, Pallas kernels, local_block(): pl.pallas_call(functools.partial(_kernel, cfg), out_shape=out_shape, in_s...  52.4 us
    pallas_call x1, Pallas kernels, local_block(): pl.pallas_call(functools.partial(_write, n_blk, blk), out_shape=finals, i...  2.88 us

profile of v8, /device:TPU:97, one launch (start us, length us, event | category | flops | bytes accessed | tf_op | source)
XLA Modules:
  0.0 56.1 jit_solution(9611646017557746193)
XLA Ops:
  0.6 52.4 %shard_map.126 = (bf16[4,1024,384]{2,1,0:T(8,128)(2,1)S(1)}, bf16[4,1024,384]{2,1,0:T(8,128)(2,1)S(1)}, f32[48,1152]{1,0:T(8,128)S(1)}, f32[48,384]{1,0:T(8,128)...) custom-call(bf16[1,4096,384]{2,1,0:T(8,128)(2,1)} %x_hbm.1, bf16[1,4096,384]{2,1,0:T(8,128)(2,1)} %gy_hbm.1, ...), custom_call_target="tpu_custom_call" | custom-call | tf_op jit(solution)/shard_map/pallas_call | solution.py:668
  53.0 2.9 %shard_map.127 = (bf16[1,4096,384]{2,1,0:T(8,128)(2,1)}, bf16[1,4096,384]{2,1,0:T(8,128)(2,1)}, f32[48,1152]{1,0:T(8,128)}, f32[48,384]{1,0:T(8,128)}, f32[384]{0:T(512)}, /*index=5*/f32[384]{0:T(512)}, f32[8]{0:T(128)}) custom-call(bf16[4,1024,384]{2,1,0:T(8,128)(2,1)S(1)} %get-tuple-element.14.refs_0_, ...), custom_call_target="tpu_custom_call" | custom-call | tf_op jit(solution)/shard_map/pallas_call | solution.py:683
